TPU v7x, 128 devices: a whole 4x4x4 slice. The times are simulated.
128 devices in a mesh: gz: 16 (over z_hi, x, core), gy: 8 (over z_lo, y).
Axes of the slice: x: 4, y: 4, z: 4 (z_hi: 2, z_lo: 2; z = z_hi * 2 + z_lo), core: 2. Of those that a mesh axis runs over, the one named last changes fastest.
Arguments:
- source: float32 [512, 256, 256], P(('gz', 'gy')), may hold values from -8 to 8
- vertical: float32 [512], P(('gz', 'gy')), may hold values from 1 to 64
- reaction: float32 [512, 256, 256], P(('gz', 'gy')), may hold values from 0.05 to 2
Outputs:
- solution: float32 [512, 256, 256], P(('gz', 'gy'))
- norms: float32 [2], replicated
All inputs are finite; a program needn't handle non-finite values.
Results may differ from a plain program's by a relative error of at most 0.0001.
Values sent between devices are 32-bit elements; how exact they have to be, the bound alone decides.
A program may use at most 192 MiB of HBM per device.

v0:
```python
import functools

import jax
import jax.numpy as jnp
from jax import lax
from jax.experimental import pallas as pl
from jax.experimental.pallas import tpu as pltpu
from jax.sharding import PartitionSpec as P

F32 = jnp.float32
MESH = pl.DeviceIdType.MESH
CYCLES = 2
STEPS = 9
EVENTS = 11
OMEGA = 0.8
H = (1.0, 0.25, 1.0 / 16, 1.0 / 64, 1.0 / 256)
GROUP_Z = 16
GROUP_Y = 8
DEVICES = 128
PAD = 8


def snake_wide(g):
    high, quarter, core = lax.div(g, 8), lax.div(lax.rem(g, 8), 2), lax.rem(g, 2)
    return high * 8 + 2 * (quarter + high * (3 - 2 * quarter)) + core


def snake_narrow(g):
    high, quarter = lax.div(g, 4), lax.rem(g, 4)
    return high * 4 + quarter + high * (3 - 2 * quarter)


def dot(a, b):
    return jnp.dot(a, b, preferred_element_type=F32, precision=lax.Precision.HIGHEST)


def roll_lanes(v, s):
    return pltpu.roll(v, s % 128, 1)


def roll_rows(v, s):
    return pltpu.roll(v, s % 8, 0)


def lane_iota():
    return lax.broadcasted_iota(jnp.int32, (8, 128), 1)


def row_iota():
    return lax.broadcasted_iota(jnp.int32, (8, 128), 0)


def below(v, s):
    if s < 4:
        inner = lane_iota() % 4 >= s
        return [
            jnp.where(inner, roll_lanes(v[g], s), roll_lanes(v[g - 1], s - 4 if g else s + 4))
            for g in range(8)
        ]
    if s < 32:
        t = s // 4
        return [v[g - t] if g >= t else roll_lanes(v[g - t + 8], 8) for g in range(8)]
    return [roll_lanes(v[g], s // 4) for g in range(8)]


def above(v, s):
    if s < 4:
        inner = lane_iota() % 4 < 4 - s
        return [
            jnp.where(
                inner,
                roll_lanes(v[g], -s),
                roll_lanes(v[(g + 1) % 8], 4 - s if g < 7 else -4 - s),
            )
            for g in range(8)
        ]
    if s < 32:
        t = s // 4
        return [v[g + t] if g + t < 8 else roll_lanes(v[g + t - 8], -8) for g in range(8)]
    return [roll_lanes(v[g], -(s // 4)) for g in range(8)]


def kernel(
    source, vertical, reaction, out, norms,
    vb, g0, d0, j0, r0, wb, g1, d1, j1, r1, e1, compact, spread, lhs,
    send_as, recv_as, send_bs, recv_bs, send_a, recv_a, send_b, recv_b,
    back_b, got_b, back_a, got_a, grown,
    dl, vl, cf, val, hx, hy, ys, rhs2, rhs3, res,
    nacc, nb, nz,
    in_sem, z_send, z_recv, as_send, as_recv, bs_send, bs_recv, a_send, a_recv, b_send, b_recv,
    bb_send, bb_recv, ba_send, ba_recv, h_send, h_recv, n_send, n_recv,
):
    gz, gy = lax.axis_index("gz"), lax.axis_index("gy")
    me = gz * GROUP_Y + gy
    wide, narrow = snake_wide(gz), snake_narrow(gy)

    def device(d):
        d = lax.rem(d + DEVICES, DEVICES)
        return (lax.div(d, GROUP_Y), lax.rem(d, GROUP_Y))

    loads = []
    for p in range(4):
        for half in range(2):
            lanes = pl.ds(half * 128, 128)
            loads.append(pltpu.make_async_copy(source.at[p, :, lanes], g0.at[p, half], in_sem.at[0, p, half]))
            loads.append(pltpu.make_async_copy(reaction.at[p, :, lanes], r0.at[p, half], in_sem.at[1, p, half]))
    for copy in loads:
        copy.start()

    @pl.loop(0, 12)
    def _(i):
        for half in range(2):
            vb[lax.div(i, 6), lax.rem(i, 6), half] = jnp.zeros((256 + 2 * PAD, 128), F32)
        wb[lax.div(i, 6), lax.rem(i, 6)] = jnp.zeros((128 + 2 * PAD, 128), F32)

    @pl.when(wide == 0)
    def _():
        for e in range(EVENTS):
            hx[e, 0] = jnp.zeros((64, 128), F32)

    @pl.when(wide == GROUP_Z - 1)
    def _():
        for e in range(EVENTS):
            hx[e, 1] = jnp.zeros((64, 128), F32)

    @pl.when(narrow == 0)
    def _():
        for e in range(EVENTS):
            hy[e, 0] = jnp.zeros((16, 128), F32)

    @pl.when(narrow == GROUP_Y - 1)
    def _():
        for e in range(EVENTS):
            hy[e, 1] = jnp.zeros((16, 128), F32)

    from_lane = lax.broadcasted_iota(jnp.int32, (128, 128), 0)
    to_lane = lax.broadcasted_iota(jnp.int32, (128, 128), 1)
    for half in range(2):
        compact[half] = jnp.where(to_lane == 64 * half + from_lane // 2, 0.25, 0.0).astype(F32)
        spread[half] = jnp.where(from_lane == 64 * half + to_lane // 2, 1.0, 0.0).astype(F32)

    barrier = pltpu.get_barrier_semaphore()
    for k in range(1, GROUP_Z):
        pl.semaphore_signal(barrier, inc=1, device_id=(lax.rem(gz + k, GROUP_Z), gy), device_id_type=MESH)
    for k in range(1, GROUP_Y):
        pl.semaphore_signal(barrier, inc=1, device_id=(gz, lax.rem(gy + k, GROUP_Y)), device_id_type=MESH)

    rim = jnp.logical_or(gy == 0, gy == GROUP_Y - 1)

    @pl.when(gy == 0)
    def _():
        pl.semaphore_signal(barrier, inc=1, device_id=device(me - 1), device_id_type=MESH)

    @pl.when(gy == GROUP_Y - 1)
    def _():
        pl.semaphore_signal(barrier, inc=1, device_id=device(me + 1), device_id_type=MESH)

    pl.semaphore_wait(barrier, GROUP_Z + GROUP_Y - 2 + rim.astype(jnp.int32))

    def line_up(first, last, low, high, level, slot):
        up = pltpu.make_async_remote_copy(
            src_ref=last, dst_ref=low, send_sem=z_send.at[level, slot, 0],
            recv_sem=z_recv.at[level, slot, 0], device_id=device(me + 1), device_id_type=MESH,
        )
        down = pltpu.make_async_remote_copy(
            src_ref=first, dst_ref=high, send_sem=z_send.at[level, slot, 1],
            recv_sem=z_recv.at[level, slot, 1], device_id=device(me - 1), device_id_type=MESH,
        )

        @pl.when(me < DEVICES - 1)
        def _():
            up.start()

        @pl.when(me > 0)
        def _():
            down.start()

        @pl.when(me < DEVICES - 1)
        def _():
            up.wait_send()
            down.wait_recv()

        @pl.when(me > 0)
        def _():
            down.wait_send()
            up.wait_recv()

    def exchange0(slot):
        rows = pl.ds(PAD, 256)
        line_up(
            vb.at[slot, 1, :, rows], vb.at[slot, 4, :, rows],
            vb.at[slot, 0, :, rows], vb.at[slot, 5, :, rows], 0, slot,
        )

    def exchange1(slot):
        rows = pl.ds(PAD, 128)
        line_up(
            wb.at[slot, 1, rows], wb.at[slot, 4, rows], wb.at[slot, 0, rows], wb.at[slot, 5, rows],
            1, slot,
        )

    def all_wide(src, pick, dst, place, send_sem, recv_sem):
        copies = []
        for k in range(1, GROUP_Z):
            peer = lax.rem(gz + k, GROUP_Z)
            copies.append(
                pltpu.make_async_remote_copy(
                    src_ref=src.at[pick(peer)], dst_ref=dst.at[place], send_sem=send_sem.at[k],
                    recv_sem=recv_sem.at[k], device_id=(peer, gy), device_id_type=MESH,
                )
            )
        for copy in copies:
            copy.start()
        dst[place] = src[pick(gz)]
        for copy in copies:
            copy.wait()

    def all_narrow(src, pick, dst, place, send_sem, recv_sem):
        copies = []
        for k in range(1, GROUP_Y):
            peer = lax.rem(gy + k, GROUP_Y)
            copies.append(
                pltpu.make_async_remote_copy(
                    src_ref=src.at[pick(peer)], dst_ref=dst.at[place], send_sem=send_sem.at[k],
                    recv_sem=recv_sem.at[k], device_id=(gz, peer), device_id_type=MESH,
                )
            )
        for copy in copies:
            copy.start()
        dst[place] = src[pick(gy)]
        for copy in copies:
            copy.wait()

    BLOCK = 32
    lanes0 = lax.broadcasted_iota(jnp.int32, (BLOCK, 128), 1)

    def around0(slot, p, row):
        rows = pl.ds(PAD + row, BLOCK)
        centre = [vb[slot, p + 1, half, rows, :] for half in range(2)]
        left = [pltpu.roll(c, 1, 1) for c in centre]
        right = [pltpu.roll(c, 127, 1) for c in centre]
        sums = [
            jnp.where(lanes0 == 0, 0.0, left[0]) + jnp.where(lanes0 == 127, right[1], right[0]),
            jnp.where(lanes0 == 0, left[0], left[1]) + jnp.where(lanes0 == 127, 0.0, right[1]),
        ]
        coupled = vertical[p]
        total = []
        for half in range(2):
            beside = vb[slot, p + 1, half, pl.ds(PAD + row - 1, BLOCK), :]
            beside = beside + vb[slot, p + 1, half, pl.ds(PAD + row + 1, BLOCK), :]
            along = vb[slot, p, half, rows, :] + vb[slot, p + 2, half, rows, :]
            total.append(H[0] * (sums[half] + beside) + coupled * along)
        return centre, total

    def sweep0(old, new):
        @pl.loop(0, 4)
        def _(p):
            for row in range(0, 256, BLOCK):
                centre, total = around0(old, p, row)
                rows = pl.ds(row, BLOCK)
                for half in range(2):
                    fresh = (1.0 - OMEGA) * centre[half] + j0[p, half, rows, :] * (g0[p, half, rows, :] + total[half])
                    vb[new, p + 1, half, pl.ds(PAD + row, BLOCK), :] = fresh

    def residual0(slot, keep, sums):
        @pl.loop(0, 4)
        def _(p):
            for row in range(0, 256, BLOCK):
                centre, total = around0(slot, p, row)
                rows = pl.ds(row, BLOCK)
                for half in range(2):
                    left = g0[p, half, rows, :] + total[half] - d0[p, half, rows, :] * centre[half]
                    if keep:
                        r0[p, half, rows, :] = left
                    else:
                        nacc[sums] += (left * left).reshape(BLOCK // 8, 8, 128).sum(axis=0)

    lanes1 = lax.broadcasted_iota(jnp.int32, (BLOCK, 128), 1)

    def around1(slot, p, row):
        rows = pl.ds(PAD + row, BLOCK)
        centre = wb[slot, p + 1, rows, :]
        sums = jnp.where(lanes1 == 0, 0.0, pltpu.roll(centre, 1, 1))
        sums = sums + jnp.where(lanes1 == 127, 0.0, pltpu.roll(centre, 127, 1))
        sums = sums + wb[slot, p + 1, pl.ds(PAD + row - 1, BLOCK), :]
        sums = sums + wb[slot, p + 1, pl.ds(PAD + row + 1, BLOCK), :]
        along = wb[slot, p, rows, :] + wb[slot, p + 2, rows, :]
        return centre, H[1] * sums + vertical[p] * along

    def sweep1(old, store):
        @pl.loop(0, 4)
        def _(p):
            for row in range(0, 128, BLOCK):
                centre, total = around1(old, p, row)
                rows = pl.ds(row, BLOCK)
                store(p, row, (1.0 - OMEGA) * centre + j1[p, rows, :] * (g1[p, rows, :] + total))

    def store_second(p, row, fresh):
        wb[1, p + 1, pl.ds(PAD + row, BLOCK), :] = fresh

    def store_error(p, row, fresh):
        e1[p, pl.ds(row, BLOCK), :] = fresh

    def residual1():
        @pl.loop(0, 4)
        def _(p):
            for row in range(0, 128, BLOCK):
                centre, total = around1(1, p, row)
                rows = pl.ds(row, BLOCK)
                r1[p, rows, :] = g1[p, rows, :] + total - d1[p, rows, :] * centre

    def shrink0(src, dst):
        @pl.loop(0, 4)
        def _(p):
            total = jnp.zeros((128, 128), F32)
            for half in range(2):
                pairs = src[p, half, pl.ds(0, 128, 2), :] + src[p, half, pl.ds(1, 128, 2), :]
                total = total + dot(pairs, compact[half])
            dst[p] = total

    def shrink1(src):
        total = jnp.zeros((128, 128), F32)
        for a in range(2):
            for b in range(2):
                for p in range(4):
                    first = 4 * a + 2 * b
                    pairs = src[p, pl.ds(first, 16, 8), :] + src[p, pl.ds(first + 1, 16, 8), :]
                    lhs[a, pl.ds(b * 4 + p, 16, 8), :] = pairs
            total = total + dot(lhs[a], compact[a])
        return total

    for copy in loads:
        copy.wait()
    shrink0(r0, r1)

    @pl.loop(0, 4)
    def _(p):
        coupled = 2.0 * vertical[p]
        for half in range(2):
            for row in range(0, 256, 64):
                rows = pl.ds(row, 64)
                diagonal = coupled + 4.0 * H[0] + r0[p, half, rows, :]
                d0[p, half, rows, :] = diagonal
                j0[p, half, rows, :] = OMEGA / diagonal
        diagonal = coupled + 4.0 * H[1] + r1[p]
        d1[p] = diagonal
        j1[p] = OMEGA / diagonal

    send_as[:, 0:8, :] = shrink1(r1).reshape(16, 8, 128)
    plane = row_iota() % 4
    coupling = jnp.zeros((8, 128), F32)
    for p in range(4):
        coupling = jnp.where(plane == p, vertical[p], coupling)
    for x in range(16):
        send_as[x, 8:16, :] = coupling
    all_wide(send_as, snake_wide, recv_as, gz, as_send, as_recv)
    for f in range(2):
        turned = recv_as[:, 8 * f : 8 * f + 8, :].reshape(128, 128).T
        for a in range(2):
            send_bs[:, 2 * f + a] = turned[64 * a : 64 * a + 64].reshape(8, 8, 128)
    all_narrow(send_bs, snake_narrow, recv_bs, gy, bs_send, bs_recv)

    lane, row = lane_iota(), row_iota()
    odd_x = lax.div(lax.rem(lane, 8), 4) == 1

    def tile(g):
        return pl.ds(8 * g, 8)

    def shrink2(v):
        result = []
        for a in range(2):
            mine = []
            for g in range(8):
                t = v[a][g]
                t = t + jnp.where(odd_x, roll_lanes(t, 4), roll_lanes(t, -4))
                t = t + jnp.where(row % 2 == 1, roll_rows(t, 1), roll_rows(t, -1))
                mine.append(0.25 * t)
            result.append(mine)
        return result

    def shrink3(v):
        mine = []
        for g in range(8):
            t = v[0][g] + v[1][g]
            t = t + jnp.where(row % 4 >= 2, roll_rows(t, 2), roll_rows(t, -2))
            mine.append(0.25 * t)
        return [mine]

    couplings = [recv_bs[g, 2] for g in range(8)]
    for g in range(8):
        first = jnp.where(jnp.logical_and(lane < 8, lane % 4 == 0), 0.0, couplings[g]) if g == 0 else couplings[g]
        last = jnp.where(jnp.logical_and(lane >= 120, lane % 4 == 3), 0.0, couplings[g]) if g == 7 else couplings[g]
        vl[0, tile(g), :] = first
        vl[1, tile(g), :] = last
    react2 = [[recv_bs[g, a] for g in range(8)] for a in range(2)]
    react3 = shrink2(react2)
    react4 = shrink3(react3)
    for i, (level, lines) in enumerate(((2, react2[0]), (2, react2[1]), (3, react3[0]), (3, react3[1]), (4, react4[0]))):
        for g in range(8):
            dl[i, tile(g), :] = 2.0 * couplings[g] + 4.0 * H[level] + lines[g]

    @pl.loop(0, 5)
    def _(i):
        low = [-vl[0, tile(g), :] for g in range(8)]
        high = [-vl[1, tile(g), :] for g in range(8)]
        middle = [dl[i, tile(g), :] for g in range(8)]
        for k in range(STEPS):
            s = 1 << k
            middle_below, middle_above = below(middle, s), above(middle, s)
            left = [-low[g] / middle_below[g] for g in range(8)]
            right = [-high[g] / middle_above[g] for g in range(8)]
            for g in range(8):
                cf[i, 2 * k, tile(g), :] = left[g]
                cf[i, 2 * k + 1, tile(g), :] = right[g]
            high_below, low_above = below(high, s), above(low, s)
            middle = [middle[g] + left[g] * high_below[g] + right[g] * low_above[g] for g in range(8)]
            if k < STEPS - 1:
                low_below, high_above = below(low, s), above(high, s)
                low = [left[g] * low_below[g] for g in range(8)]
                high = [right[g] * high_above[g] for g in range(8)]
        for g in range(8):
            cf[i, 2 * STEPS, tile(g), :] = 1.0 / middle[g]

    first_of = {2: 0, 3: 2, 4: 4}
    count_of = {2: 2, 3: 2, 4: 1}

    def solve(level, right):
        solved = []
        for a in range(count_of[level]):
            i = first_of[level] + a
            r = right[a]
            for k in range(STEPS):
                s = 1 << k
                down, up = below(r, s), above(r, s)
                r = [
                    r[g] + cf[i, 2 * k, tile(g), :] * down[g] + cf[i, 2 * k + 1, tile(g), :] * up[g]
                    for g in range(8)
                ]
            solved.append([r[g] * cf[i, 2 * STEPS, tile(g), :] for g in range(8)])
        return solved

    def around(level, event, v):
        count = count_of[level]
        for a in range(count):
            for g in range(8):
                val[event, pl.ds((a * 8 + g) * 8, 8), :] = v[a][g]
        size = 8 * count
        ys[event, 0, 0:size, :] = val[event, pl.ds(0, size, 8), :]
        ys[event, 1, 0:size, :] = val[event, pl.ds(7, size, 8), :]
        ends = pl.ds(0, size)
        copies = []
        for side, src, dst, there in (
            (0, val.at[event, pl.ds(64 * (count - 1), 64)], hx.at[event, 0], (snake_wide(wide + 1), gy)),
            (1, val.at[event, pl.ds(0, 64)], hx.at[event, 1], (snake_wide(wide - 1), gy)),
            (2, ys.at[event, 1, ends], hy.at[event, 0, ends], (gz, snake_narrow(narrow + 1))),
            (3, ys.at[event, 0, ends], hy.at[event, 1, ends], (gz, snake_narrow(narrow - 1))),
        ):
            copies.append(
                pltpu.make_async_remote_copy(
                    src_ref=src, dst_ref=dst, send_sem=h_send.at[event, side],
                    recv_sem=h_recv.at[event, side], device_id=there, device_id_type=MESH,
                )
            )
        has = (wide < GROUP_Z - 1, wide > 0, narrow < GROUP_Y - 1, narrow > 0)
        for side in range(4):
            pl.when(has[side])(copies[side].start)
        for side in range(4):
            pl.when(has[side])(copies[side].wait_send)
            pl.when(has[side])(copies[side ^ 1].wait_recv)
        result = []
        for a in range(count):
            mine = []
            for g in range(8):
                left, right = hx[event, 0, tile(g), :], hx[event, 1, tile(g), :]
                if level == 2:
                    both = v[0][g] + v[1][g]
                    inner, outer = (both, left + v[0][g]) if a == 0 else (v[1][g] + right, both)
                    total = jnp.where(odd_x, roll_lanes(inner, 4), roll_lanes(outer, -4))
                elif level == 3:
                    total = left + v[1][g] if a == 0 else v[0][g] + right
                else:
                    total = left + right
                low = jnp.broadcast_to(hy[event, 0, pl.ds(a * 8 + g, 1), :], (8, 128))
                high = jnp.broadcast_to(hy[event, 1, pl.ds(a * 8 + g, 1), :], (8, 128))
                shift = 1 << (level - 2)
                total = total + jnp.where(row < shift, low, roll_rows(v[a][g], shift))
                total = total + jnp.where(row >= 8 - shift, high, roll_rows(v[a][g], -shift))
                mine.append(total)
            result.append(mine)
        return result

    def relax(level, target, total):
        return solve(
            level,
            [
                [target[a][g] + H[level] * total[a][g] for g in range(8)]
                for a in range(count_of[level])
            ],
        )

    def residual(level, target, v, total):
        result = []
        for a in range(count_of[level]):
            down, up = below(v[a], 1), above(v[a], 1)
            result.append([
                target[a][g] + H[level] * total[a][g] - dl[first_of[level] + a, tile(g), :] * v[a][g]
                + vl[0, tile(g), :] * down[g] + vl[1, tile(g), :] * up[g]
                for g in range(8)
            ])
        return result

    def load(ref, count):
        return [[ref[a, tile(g), :] for g in range(8)] for a in range(count)]

    def keep(ref, v):
        for a in range(len(v)):
            for g in range(8):
                ref[a, tile(g), :] = v[a][g]

    def lines():
        target2 = lambda: [[recv_b[g, a] for g in range(8)] for a in range(2)]
        v = solve(2, target2())
        v = relax(2, target2(), around(2, 0, v))
        r = residual(2, target2(), v, around(2, 1, v))
        keep(rhs2, v)
        keep(rhs3, shrink2(r))
        target3 = lambda: load(rhs3, 2)
        v = solve(3, target3())
        v = relax(3, target3(), around(3, 2, v))
        r = residual(3, target3(), v, around(3, 3, v))
        keep(res, v)
        target4 = shrink3(r)
        v = solve(4, target4)
        for e in range(3):
            v = relax(4, target4, around(4, 4 + e, v))
        w = load(res, 2)
        v = [[w[a][g] + v[0][g] for g in range(8)] for a in range(2)]
        v = relax(3, target3(), around(3, 7, v))
        v = relax(3, target3(), around(3, 8, v))
        w = load(rhs2, 2)
        v = [[w[a][g] + v[a][g] for g in range(8)] for a in range(2)]
        v = relax(2, target2(), around(2, 9, v))
        v = relax(2, target2(), around(2, 10, v))
        for a in range(2):
            for g in range(8):
                back_b[g, a] = v[a][g]

    nacc[...] = jnp.zeros((CYCLES, 8, 128), F32)

    @pl.loop(0, CYCLES)
    def _(cycle):
        this = lax.rem(cycle, 2)
        other = 1 - this
        sweep0(this, other)
        exchange0(other)
        sweep0(other, this)
        exchange0(this)
        residual0(this, True, 0)
        shrink0(r0, g1)

        @pl.loop(0, 4)
        def _(p):
            wb[0, p + 1, pl.ds(PAD, 128), :] = j1[p] * g1[p]

        exchange1(0)
        sweep1(0, store_second)
        exchange1(1)
        residual1()

        send_a[...] = shrink1(r1).reshape(16, 8, 128)
        all_wide(send_a, snake_wide, recv_a, gz, a_send, a_recv)
        turned = recv_a[...].reshape(128, 128).T
        for a in range(2):
            send_b[:, a] = turned[64 * a : 64 * a + 64].reshape(8, 8, 128)
        all_narrow(send_b, snake_narrow, recv_b, gy, b_send, b_recv)
        lines()
        all_narrow(back_b, lambda g: g, got_b, narrow, bb_send, bb_recv)
        turned = jnp.concatenate([got_b[:, a].reshape(64, 128) for a in range(2)], axis=0).T
        back_a[...] = turned.reshape(16, 8, 128)
        all_wide(back_a, lambda g: g, got_a, wide, ba_send, ba_recv)

        @pl.loop(0, 4)
        def _(p):
            wb[0, p + 1, pl.ds(PAD, 128), :] = wb[1, p + 1, pl.ds(PAD, 128), :]

        for a in range(2):
            grown[a] = dot(got_a[...].reshape(128, 128), spread[a])
        for a in range(2):
            for b in range(2):
                for p in range(4):
                    piece = grown[a, pl.ds(b * 4 + p, 16, 8), :]
                    for i in range(2):
                        rows = pl.ds(PAD + 4 * a + 2 * b + i, 16, 8)
                        wb[0, p + 1, rows, :] = wb[0, p + 1, rows, :] + piece
        exchange1(0)
        sweep1(0, store_second)
        exchange1(1)
        sweep1(1, store_error)

        @pl.loop(0, 4)
        def _(p):
            for half in range(2):
                piece = dot(e1[p], spread[half])
                for i in range(2):
                    rows = pl.ds(PAD + i, 128, 2)
                    vb[other, p + 1, half, rows, :] = vb[this, p + 1, half, rows, :] + piece

        exchange0(other)
        sweep0(other, this)
        exchange0(this)
        sweep0(this, other)
        exchange0(other)
        residual0(other, False, cycle)

    stores = []
    for p in range(4):
        for half in range(2):
            stores.append(
                pltpu.make_async_copy(
                    vb.at[CYCLES % 2, p + 1, half, pl.ds(PAD, 256)],
                    out.at[p, :, pl.ds(half * 128, 128)],
                    in_sem.at[0, p, half],
                )
            )
    for copy in stores:
        copy.start()

    all_narrow_sum(nacc, nb, gz, gy, n_send, n_recv)
    total = nb[0]
    for g in range(1, GROUP_Y):
        total = total + nb[g]
    nacc[...] = total
    all_wide_sum(nacc, nz, gz, gy, n_send, n_recv)
    total = nz[0]
    for g in range(1, GROUP_Z):
        total = total + nz[g]
    for c in range(CYCLES):
        norms[c] = jnp.sum(total[c]) * (1.0 / (512 * 256 * 256))
    for copy in stores:
        copy.wait()


def all_narrow_sum(src, dst, gz, gy, send_sem, recv_sem):
    copies = []
    for k in range(1, GROUP_Y):
        peer = lax.rem(gy + k, GROUP_Y)
        copies.append(
            pltpu.make_async_remote_copy(
                src_ref=src, dst_ref=dst.at[gy], send_sem=send_sem.at[0, k],
                recv_sem=recv_sem.at[0, k], device_id=(gz, peer), device_id_type=MESH,
            )
        )
    for copy in copies:
        copy.start()
    dst[gy] = src[...]
    for copy in copies:
        copy.wait()


def all_wide_sum(src, dst, gz, gy, send_sem, recv_sem):
    copies = []
    for k in range(1, GROUP_Z):
        peer = lax.rem(gz + k, GROUP_Z)
        copies.append(
            pltpu.make_async_remote_copy(
                src_ref=src, dst_ref=dst.at[gz], send_sem=send_sem.at[1, k],
                recv_sem=recv_sem.at[1, k], device_id=(peer, gy), device_id_type=MESH,
            )
        )
    for copy in copies:
        copy.start()
    dst[gz] = src[...]
    for copy in copies:
        copy.wait()


def vmem(*shape):
    return pltpu.VMEM(shape, F32)


def shards(source, vertical, reaction):
    dma = pltpu.SemaphoreType.DMA
    solved, norms = pl.pallas_call(
        kernel,
        out_shape=(
            jax.ShapeDtypeStruct((4, 256, 256), F32),
            jax.ShapeDtypeStruct((CYCLES,), F32),
        ),
        in_specs=[
            pl.BlockSpec(memory_space=pl.ANY),
            pl.BlockSpec(memory_space=pltpu.SMEM),
            pl.BlockSpec(memory_space=pl.ANY),
        ],
        out_specs=(pl.BlockSpec(memory_space=pl.ANY), pl.BlockSpec(memory_space=pltpu.SMEM)),
        scratch_shapes=[
            vmem(2, 6, 2, 256 + 2 * PAD, 128),
            vmem(4, 2, 256, 128),
            vmem(4, 2, 256, 128),
            vmem(4, 2, 256, 128),
            vmem(4, 2, 256, 128),
            vmem(2, 6, 128 + 2 * PAD, 128),
            vmem(4, 128, 128),
            vmem(4, 128, 128),
            vmem(4, 128, 128),
            vmem(4, 128, 128),
            vmem(4, 128, 128),
            vmem(2, 128, 128),
            vmem(2, 128, 128),
            vmem(2, 128, 128),
            vmem(16, 16, 128),
            vmem(16, 16, 128),
            vmem(8, 4, 8, 128),
            vmem(8, 4, 8, 128),
            vmem(16, 8, 128),
            vmem(16, 8, 128),
            vmem(8, 2, 8, 128),
            vmem(8, 2, 8, 128),
            vmem(8, 2, 8, 128),
            vmem(8, 2, 8, 128),
            vmem(16, 8, 128),
            vmem(16, 8, 128),
            vmem(2, 128, 128),
            vmem(5, 64, 128),
            vmem(2, 64, 128),
            vmem(5, 2 * STEPS + 1, 64, 128),
            vmem(EVENTS, 128, 128),
            vmem(EVENTS, 2, 64, 128),
            vmem(EVENTS, 2, 16, 128),
            vmem(EVENTS, 2, 16, 128),
            vmem(2, 64, 128),
            vmem(2, 64, 128),
            vmem(2, 64, 128),
            vmem(CYCLES, 8, 128),
            vmem(GROUP_Y, CYCLES, 8, 128),
            vmem(GROUP_Z, CYCLES, 8, 128),
            dma((2, 4, 2)),
            dma((2, 2, 2)),
            dma((2, 2, 2)),
            dma((GROUP_Z,)),
            dma((GROUP_Z,)),
            dma((GROUP_Y,)),
            dma((GROUP_Y,)),
            dma((GROUP_Z,)),
            dma((GROUP_Z,)),
            dma((GROUP_Y,)),
            dma((GROUP_Y,)),
            dma((GROUP_Y,)),
            dma((GROUP_Y,)),
            dma((GROUP_Z,)),
            dma((GROUP_Z,)),
            dma((EVENTS, 4)),
            dma((EVENTS, 4)),
            dma((2, GROUP_Z)),
            dma((2, GROUP_Z)),
        ],
        compiler_params=pltpu.CompilerParams(
            collective_id=0, has_side_effects=True, vmem_limit_bytes=48 * 1024 * 1024
        ),
    )(source, vertical, reaction)
    return solved, norms


def solution(mesh):
    planes = P(("gz", "gy"), None, None)
    return jax.shard_map(
        shards,
        mesh=mesh,
        in_specs=(planes, P(("gz", "gy")), planes),
        out_specs=(planes, P()),
        check_vma=False,
    )
```

profile of v0, /device:TPU:1, one launch (start us, length us, event | category | flops | bytes accessed | tf_op | source)
XLA Modules:
  0.0 315.9 jit_solution(3262079499773176673)
XLA Ops:
  0.6 0.0 copy-start
  0.6 1.2 copy-done
  1.9 0.0 copy-start.1
  1.9 1.2 copy-done.1
  3.1 0.0 copy-start.2
  3.1 0.7 copy-done.2
  3.7 310.7 %shard_map.50 = (f32[4,256,256]{2,1,0:T(8,128)S(1)}, f32[2]{0:T(128)S(1)}) custom-call(f32[4,256,256]{2,1,0:T(8,128)S(1)} %copy-done, f32[4]{0:T(128)S(1)} %copy-done.2, f32[4,256,256]{2,1,0:T(8,128)S(1)} %copy-done.1), custom_call_target="tpu_custom_call" | custom-call | tf_op jit(solution)/shard_map/pallas_call | solution.py:683
  314.4 1.0 copy.7
  315.4 0.5 copy.8
Async XLA Ops:
  0.6 1.2 copy-start
  1.9 1.2 copy-start.1
  3.1 0.7 copy-start.2
where the time goes:
time: 316 us
  Pallas kernels  311 us (98%)
  local copies, waits for them, and re-layouts  4.58 us (1%)
    pallas_call x1, Pallas kernels, shards(): pl.pallas_call(kernel, out_shape=(jax.ShapeDtypeStruct((4, 256, 256), F32...  311 us

commit v1 on v0

--- a/solution.py
+++ b/solution.py
@@ -31,7 +31,14 @@
 
 
 def dot(a, b):
-    return jnp.dot(a, b, preferred_element_type=F32, precision=lax.Precision.HIGHEST)
+    total = None
+    for part in range(3):
+        piece = a.astype(jnp.bfloat16)
+        product = jnp.dot(piece, b, preferred_element_type=F32)
+        total = product if total is None else total + product
+        if part < 2:
+            a = a - piece.astype(F32)
+    return total
 
 
 def roll_lanes(v, s):
@@ -82,12 +89,13 @@
 
 def kernel(
     source, vertical, reaction, out, norms,
-    vb, g0, d0, j0, r0, wb, g1, d1, j1, r1, e1, compact, spread, lhs,
+    vb, g0, d0, j0, r0, vt, wb, g1, d1, j1, r1, e1, compact, spread, lhs,
     send_as, recv_as, send_bs, recv_bs, send_a, recv_a, send_b, recv_b,
-    back_b, got_b, back_a, got_a, grown,
+    back_b, got_b, back_a, got_a, beyond, ends, grown,
     dl, vl, cf, val, hx, hy, ys, rhs2, rhs3, res,
     nacc, nb, nz,
-    in_sem, z_send, z_recv, as_send, as_recv, bs_send, bs_recv, a_send, a_recv, b_send, b_recv,
+    in_sem, z_send, z_recv, c_send, c_recv,
+    as_send, as_recv, bs_send, bs_recv, a_send, a_recv, b_send, b_recv,
     bb_send, bb_recv, ba_send, ba_recv, h_send, h_recv, n_send, n_recv,
 ):
     gz, gy = lax.axis_index("gz"), lax.axis_index("gy")
@@ -102,16 +110,48 @@
     for p in range(4):
         for half in range(2):
             lanes = pl.ds(half * 128, 128)
-            loads.append(pltpu.make_async_copy(source.at[p, :, lanes], g0.at[p, half], in_sem.at[0, p, half]))
+            loads.append(pltpu.make_async_copy(source.at[p, :, lanes], g0.at[p + 2, half], in_sem.at[0, p, half]))
             loads.append(pltpu.make_async_copy(reaction.at[p, :, lanes], r0.at[p, half], in_sem.at[1, p, half]))
     for copy in loads:
         copy.start()
 
-    @pl.loop(0, 12)
+    @pl.loop(0, 30)
     def _(i):
         for half in range(2):
-            vb[lax.div(i, 6), lax.rem(i, 6), half] = jnp.zeros((256 + 2 * PAD, 128), F32)
-        wb[lax.div(i, 6), lax.rem(i, 6)] = jnp.zeros((128 + 2 * PAD, 128), F32)
+            for row in (0, PAD + 256):
+                vb[lax.div(i, 10), lax.rem(i, 10), half, pl.ds(row, PAD), :] = jnp.zeros((PAD, 128), F32)
+
+    @pl.loop(0, 28)
+    def _(i):
+        for row in (0, PAD + 128):
+            wb[lax.div(i, 14), lax.rem(i, 14), pl.ds(row, PAD), :] = jnp.zeros((PAD, 128), F32)
+
+    for p in range(4):
+        vt[p + 4] = jnp.full((8, 128), vertical[p], F32)
+
+    @pl.when(jnp.logical_or(me < 2, me >= DEVICES - 2))
+    def _():
+        @pl.loop(0, 30)
+        def _(i):
+            for half in range(2):
+                vb[lax.div(i, 10), lax.rem(i, 10), half] = jnp.zeros((256 + 2 * PAD, 128), F32)
+
+        @pl.loop(0, 28)
+        def _(i):
+            wb[lax.div(i, 14), lax.rem(i, 14)] = jnp.zeros((128 + 2 * PAD, 128), F32)
+
+        for i in (0, 1, 6, 7):
+            for half in range(2):
+                g0[i, half] = jnp.zeros((256, 128), F32)
+                j0[i, half] = jnp.zeros((256, 128), F32)
+        for i in (0, 1, 2, 3, 8, 9, 10, 11):
+            vt[i] = jnp.zeros((8, 128), F32)
+            g1[i] = jnp.zeros((128, 128), F32)
+            j1[i] = jnp.zeros((128, 128), F32)
+        for i in (0, 2):
+            got_a[i] = jnp.zeros((16, 8, 128), F32)
+        for i in range(2):
+            beyond[i] = jnp.zeros((32, 128), F32)
 
     @pl.when(wide == 0)
     def _():
@@ -136,8 +176,8 @@
     from_lane = lax.broadcasted_iota(jnp.int32, (128, 128), 0)
     to_lane = lax.broadcasted_iota(jnp.int32, (128, 128), 1)
     for half in range(2):
-        compact[half] = jnp.where(to_lane == 64 * half + from_lane // 2, 0.25, 0.0).astype(F32)
-        spread[half] = jnp.where(from_lane == 64 * half + to_lane // 2, 1.0, 0.0).astype(F32)
+        compact[half] = jnp.where(to_lane == 64 * half + from_lane // 2, 0.25, 0.0).astype(jnp.bfloat16)
+        spread[half] = jnp.where(from_lane == 64 * half + to_lane // 2, 1.0, 0.0).astype(jnp.bfloat16)
 
     barrier = pltpu.get_barrier_semaphore()
     for k in range(1, GROUP_Z):
@@ -145,59 +185,59 @@
     for k in range(1, GROUP_Y):
         pl.semaphore_signal(barrier, inc=1, device_id=(gz, lax.rem(gy + k, GROUP_Y)), device_id_type=MESH)
 
-    rim = jnp.logical_or(gy == 0, gy == GROUP_Y - 1)
-
-    @pl.when(gy == 0)
-    def _():
-        pl.semaphore_signal(barrier, inc=1, device_id=device(me - 1), device_id_type=MESH)
-
-    @pl.when(gy == GROUP_Y - 1)
-    def _():
-        pl.semaphore_signal(barrier, inc=1, device_id=device(me + 1), device_id_type=MESH)
-
-    pl.semaphore_wait(barrier, GROUP_Z + GROUP_Y - 2 + rim.astype(jnp.int32))
-
-    def line_up(first, last, low, high, level, slot):
-        up = pltpu.make_async_remote_copy(
-            src_ref=last, dst_ref=low, send_sem=z_send.at[level, slot, 0],
-            recv_sem=z_recv.at[level, slot, 0], device_id=device(me + 1), device_id_type=MESH,
+    for side, near, far in ((-1, 0, 1), (1, GROUP_Y - 1, GROUP_Y - 2)):
+        for edge, steps in ((near, 1), (near, 2), (far, 2)):
+
+            @pl.when(gy == edge)
+            def _(side=side, steps=steps):
+                pl.semaphore_signal(
+                    barrier, inc=1, device_id=device(me + side * steps), device_id_type=MESH
+                )
+
+    outside = 2 * jnp.logical_or(gy == 0, gy == GROUP_Y - 1).astype(jnp.int32)
+    outside = outside + jnp.logical_or(gy == 1, gy == GROUP_Y - 2).astype(jnp.int32)
+    pl.semaphore_wait(barrier, GROUP_Z + GROUP_Y - 2 + outside)
+
+    has_up, has_down = me < DEVICES - 1, me > 0
+
+    class Pair:
+        def __init__(self, up, down, send_sem, recv_sem, steps=1):
+            self.steps = steps
+            self.copies = [
+                pltpu.make_async_remote_copy(
+                    src_ref=src, dst_ref=dst, send_sem=send_sem.at[i], recv_sem=recv_sem.at[i],
+                    device_id=device(me + shift), device_id_type=MESH,
+                )
+                for i, (src, dst), shift in ((0, up, steps), (1, down, -steps))
+            ]
+
+        def start(self):
+            pl.when(me < DEVICES - self.steps)(self.copies[0].start)
+            pl.when(me >= self.steps)(self.copies[1].start)
+
+        def wait(self):
+            @pl.when(me < DEVICES - self.steps)
+            def _():
+                self.copies[0].wait_send()
+                self.copies[1].wait_recv()
+
+            @pl.when(me >= self.steps)
+            def _():
+                self.copies[1].wait_send()
+                self.copies[0].wait_recv()
+
+    def pair(i, up, down, steps=1):
+        return Pair(up, down, z_send.at[i], z_recv.at[i], steps)
+
+    def exchange0(slot, i):
+        rows = pl.ds(PAD, 256)
+        both = pair(
+            i,
+            (vb.at[slot, 6, :, rows], vb.at[slot, 2, :, rows]),
+            (vb.at[slot, 3, :, rows], vb.at[slot, 7, :, rows]),
         )
-        down = pltpu.make_async_remote_copy(
-            src_ref=first, dst_ref=high, send_sem=z_send.at[level, slot, 1],
-            recv_sem=z_recv.at[level, slot, 1], device_id=device(me - 1), device_id_type=MESH,
-        )
-
-        @pl.when(me < DEVICES - 1)
-        def _():
-            up.start()
-
-        @pl.when(me > 0)
-        def _():
-            down.start()
-
-        @pl.when(me < DEVICES - 1)
-        def _():
-            up.wait_send()
-            down.wait_recv()
-
-        @pl.when(me > 0)
-        def _():
-            down.wait_send()
-            up.wait_recv()
-
-    def exchange0(slot):
-        rows = pl.ds(PAD, 256)
-        line_up(
-            vb.at[slot, 1, :, rows], vb.at[slot, 4, :, rows],
-            vb.at[slot, 0, :, rows], vb.at[slot, 5, :, rows], 0, slot,
-        )
-
-    def exchange1(slot):
-        rows = pl.ds(PAD, 128)
-        line_up(
-            wb.at[slot, 1, rows], wb.at[slot, 4, rows], wb.at[slot, 0, rows], wb.at[slot, 5, rows],
-            1, slot,
-        )
+        both.start()
+        both.wait()
 
     def all_wide(src, pick, dst, place, send_sem, recv_sem):
         copies = []
@@ -212,8 +252,12 @@
         for copy in copies:
             copy.start()
         dst[place] = src[pick(gz)]
-        for copy in copies:
-            copy.wait()
+
+        def finish():
+            for copy in copies:
+                copy.wait()
+
+        return finish
 
     def all_narrow(src, pick, dst, place, send_sem, recv_sem):
         copies = []
@@ -228,39 +272,45 @@
         for copy in copies:
             copy.start()
         dst[place] = src[pick(gy)]
-        for copy in copies:
-            copy.wait()
+
+        def finish():
+            for copy in copies:
+                copy.wait()
+
+        return finish
 
     BLOCK = 32
     lanes0 = lax.broadcasted_iota(jnp.int32, (BLOCK, 128), 1)
 
     def around0(slot, p, row):
         rows = pl.ds(PAD + row, BLOCK)
-        centre = [vb[slot, p + 1, half, rows, :] for half in range(2)]
+        centre = [vb[slot, p + 3, half, rows, :] for half in range(2)]
         left = [pltpu.roll(c, 1, 1) for c in centre]
         right = [pltpu.roll(c, 127, 1) for c in centre]
         sums = [
             jnp.where(lanes0 == 0, 0.0, left[0]) + jnp.where(lanes0 == 127, right[1], right[0]),
             jnp.where(lanes0 == 0, left[0], left[1]) + jnp.where(lanes0 == 127, 0.0, right[1]),
         ]
-        coupled = vertical[p]
+        coupled = jnp.broadcast_to(vt[p + 4, 0:1, :], (BLOCK, 128))
         total = []
         for half in range(2):
-            beside = vb[slot, p + 1, half, pl.ds(PAD + row - 1, BLOCK), :]
-            beside = beside + vb[slot, p + 1, half, pl.ds(PAD + row + 1, BLOCK), :]
-            along = vb[slot, p, half, rows, :] + vb[slot, p + 2, half, rows, :]
+            beside = vb[slot, p + 3, half, pl.ds(PAD + row - 1, BLOCK), :]
+            beside = beside + vb[slot, p + 3, half, pl.ds(PAD + row + 1, BLOCK), :]
+            along = vb[slot, p + 2, half, rows, :] + vb[slot, p + 4, half, rows, :]
             total.append(H[0] * (sums[half] + beside) + coupled * along)
         return centre, total
 
-    def sweep0(old, new):
-        @pl.loop(0, 4)
-        def _(p):
+    def sweep0(old, new, reach):
+        @pl.loop(0, 4 + 2 * reach)
+        def _(i):
+            p = i - reach
             for row in range(0, 256, BLOCK):
                 centre, total = around0(old, p, row)
                 rows = pl.ds(row, BLOCK)
                 for half in range(2):
-                    fresh = (1.0 - OMEGA) * centre[half] + j0[p, half, rows, :] * (g0[p, half, rows, :] + total[half])
-                    vb[new, p + 1, half, pl.ds(PAD + row, BLOCK), :] = fresh
+                    fresh = g0[p + 2, half, rows, :] + total[half]
+                    fresh = (1.0 - OMEGA) * centre[half] + j0[p + 2, half, rows, :] * fresh
+                    vb[new, p + 3, half, pl.ds(PAD + row, BLOCK), :] = fresh
 
     def residual0(slot, keep, sums):
         @pl.loop(0, 4)
@@ -269,7 +319,7 @@
                 centre, total = around0(slot, p, row)
                 rows = pl.ds(row, BLOCK)
                 for half in range(2):
-                    left = g0[p, half, rows, :] + total[half] - d0[p, half, rows, :] * centre[half]
+                    left = g0[p + 2, half, rows, :] + total[half] - d0[p, half, rows, :] * centre[half]
                     if keep:
                         r0[p, half, rows, :] = left
                     else:
@@ -279,27 +329,29 @@
 
     def around1(slot, p, row):
         rows = pl.ds(PAD + row, BLOCK)
-        centre = wb[slot, p + 1, rows, :]
+        centre = wb[slot, p + 5, rows, :]
         sums = jnp.where(lanes1 == 0, 0.0, pltpu.roll(centre, 1, 1))
         sums = sums + jnp.where(lanes1 == 127, 0.0, pltpu.roll(centre, 127, 1))
-        sums = sums + wb[slot, p + 1, pl.ds(PAD + row - 1, BLOCK), :]
-        sums = sums + wb[slot, p + 1, pl.ds(PAD + row + 1, BLOCK), :]
-        along = wb[slot, p, rows, :] + wb[slot, p + 2, rows, :]
-        return centre, H[1] * sums + vertical[p] * along
-
-    def sweep1(old, store):
-        @pl.loop(0, 4)
-        def _(p):
+        sums = sums + wb[slot, p + 5, pl.ds(PAD + row - 1, BLOCK), :]
+        sums = sums + wb[slot, p + 5, pl.ds(PAD + row + 1, BLOCK), :]
+        along = wb[slot, p + 4, rows, :] + wb[slot, p + 6, rows, :]
+        return centre, H[1] * sums + jnp.broadcast_to(vt[p + 4, 0:1, :], (BLOCK, 128)) * along
+
+    def sweep1(old, store, reach):
+        @pl.loop(0, 4 + 2 * reach)
+        def _(i):
+            p = i - reach
             for row in range(0, 128, BLOCK):
                 centre, total = around1(old, p, row)
                 rows = pl.ds(row, BLOCK)
-                store(p, row, (1.0 - OMEGA) * centre + j1[p, rows, :] * (g1[p, rows, :] + total))
+                fresh = j1[p + 4, rows, :] * (g1[p + 4, rows, :] + total)
+                store(p, row, (1.0 - OMEGA) * centre + fresh)
 
     def store_second(p, row, fresh):
-        wb[1, p + 1, pl.ds(PAD + row, BLOCK), :] = fresh
+        wb[1, p + 5, pl.ds(PAD + row, BLOCK), :] = fresh
 
     def store_error(p, row, fresh):
-        e1[p, pl.ds(row, BLOCK), :] = fresh
+        e1[p + 3, pl.ds(row, BLOCK), :] = fresh
 
     def residual1():
         @pl.loop(0, 4)
@@ -307,16 +359,16 @@
             for row in range(0, 128, BLOCK):
                 centre, total = around1(1, p, row)
                 rows = pl.ds(row, BLOCK)
-                r1[p, rows, :] = g1[p, rows, :] + total - d1[p, rows, :] * centre
-
-    def shrink0(src, dst):
+                r1[p, rows, :] = g1[p + 4, rows, :] + total - d1[p, rows, :] * centre
+
+    def shrink0(src, dst, first):
         @pl.loop(0, 4)
         def _(p):
             total = jnp.zeros((128, 128), F32)
             for half in range(2):
                 pairs = src[p, half, pl.ds(0, 128, 2), :] + src[p, half, pl.ds(1, 128, 2), :]
                 total = total + dot(pairs, compact[half])
-            dst[p] = total
+            dst[p + first] = total
 
     def shrink1(src):
         total = jnp.zeros((128, 128), F32)
@@ -329,9 +381,23 @@
             total = total + dot(lhs[a], compact[a])
         return total
 
+    early = []
+    for i in range(2):
+        for half in range(2):
+            lanes = pl.ds(half * 128, 128)
+            early.append(
+                pair(
+                    4 + 2 * i + half,
+                    (source.at[2 + i, :, lanes], g0.at[i, half]),
+                    (source.at[i, :, lanes], g0.at[6 + i, half]),
+                )
+            )
+    early.append(pair(2, (vt.at[4:8], vt.at[0:4]), (vt.at[4:8], vt.at[8:12])))
+    for both in early:
+        both.start()
     for copy in loads:
         copy.wait()
-    shrink0(r0, r1)
+    shrink0(r0, r1, 0)
 
     @pl.loop(0, 4)
     def _(p):
@@ -341,10 +407,10 @@
                 rows = pl.ds(row, 64)
                 diagonal = coupled + 4.0 * H[0] + r0[p, half, rows, :]
                 d0[p, half, rows, :] = diagonal
-                j0[p, half, rows, :] = OMEGA / diagonal
+                j0[p + 2, half, rows, :] = OMEGA / diagonal
         diagonal = coupled + 4.0 * H[1] + r1[p]
         d1[p] = diagonal
-        j1[p] = OMEGA / diagonal
+        j1[p + 4] = OMEGA / diagonal
 
     send_as[:, 0:8, :] = shrink1(r1).reshape(16, 8, 128)
     plane = row_iota() % 4
@@ -353,12 +419,17 @@
         coupling = jnp.where(plane == p, vertical[p], coupling)
     for x in range(16):
         send_as[x, 8:16, :] = coupling
-    all_wide(send_as, snake_wide, recv_as, gz, as_send, as_recv)
+    all_wide(send_as, snake_wide, recv_as, gz, as_send, as_recv)()
     for f in range(2):
         turned = recv_as[:, 8 * f : 8 * f + 8, :].reshape(128, 128).T
         for a in range(2):
             send_bs[:, 2 * f + a] = turned[64 * a : 64 * a + 64].reshape(8, 8, 128)
-    all_narrow(send_bs, snake_narrow, recv_bs, gy, bs_send, bs_recv)
+    finish = all_narrow(send_bs, snake_narrow, recv_bs, gy, bs_send, bs_recv)
+    early.append(pair(8, (j0.at[4:6], j0.at[0:2]), (j0.at[2:4], j0.at[6:8])))
+    late = pair(9, (j1.at[4:8], j1.at[0:4]), (j1.at[4:8], j1.at[8:12]))
+    early[-1].start()
+    late.start()
+    finish()
 
     lane, row = lane_iota(), row_iota()
     odd_x = lax.div(lax.rem(lane, 8), 4) == 1
@@ -439,7 +510,7 @@
             solved.append([r[g] * cf[i, 2 * STEPS, tile(g), :] for g in range(8)])
         return solved
 
-    def around(level, event, v):
+    def around(level, event, v, chunks):
         count = count_of[level]
         for a in range(count):
             for g in range(8):
@@ -447,13 +518,13 @@
         size = 8 * count
         ys[event, 0, 0:size, :] = val[event, pl.ds(0, size, 8), :]
         ys[event, 1, 0:size, :] = val[event, pl.ds(7, size, 8), :]
-        ends = pl.ds(0, size)
+        span = pl.ds(0, size)
         copies = []
         for side, src, dst, there in (
             (0, val.at[event, pl.ds(64 * (count - 1), 64)], hx.at[event, 0], (snake_wide(wide + 1), gy)),
             (1, val.at[event, pl.ds(0, 64)], hx.at[event, 1], (snake_wide(wide - 1), gy)),
-            (2, ys.at[event, 1, ends], hy.at[event, 0, ends], (gz, snake_narrow(narrow + 1))),
-            (3, ys.at[event, 0, ends], hy.at[event, 1, ends], (gz, snake_narrow(narrow - 1))),
+            (2, ys.at[event, 1, span], hy.at[event, 0, span], (gz, snake_narrow(narrow + 1))),
+            (3, ys.at[event, 0, span], hy.at[event, 1, span], (gz, snake_narrow(narrow - 1))),
         ):
             copies.append(
                 pltpu.make_async_remote_copy(
@@ -464,6 +535,7 @@
         has = (wide < GROUP_Z - 1, wide > 0, narrow < GROUP_Y - 1, narrow > 0)
         for side in range(4):
             pl.when(has[side])(copies[side].start)
+        chunks[event + 2].start()
         for side in range(4):
             pl.when(has[side])(copies[side].wait_send)
             pl.when(has[side])(copies[side ^ 1].wait_recv)
@@ -517,99 +589,160 @@
             for g in range(8):
                 ref[a, tile(g), :] = v[a][g]
 
-    def lines():
+    def lines(chunks):
         target2 = lambda: [[recv_b[g, a] for g in range(8)] for a in range(2)]
         v = solve(2, target2())
-        v = relax(2, target2(), around(2, 0, v))
-        r = residual(2, target2(), v, around(2, 1, v))
+        v = relax(2, target2(), around(2, 0, v, chunks))
+        r = residual(2, target2(), v, around(2, 1, v, chunks))
         keep(rhs2, v)
         keep(rhs3, shrink2(r))
         target3 = lambda: load(rhs3, 2)
         v = solve(3, target3())
-        v = relax(3, target3(), around(3, 2, v))
-        r = residual(3, target3(), v, around(3, 3, v))
+        v = relax(3, target3(), around(3, 2, v, chunks))
+        r = residual(3, target3(), v, around(3, 3, v, chunks))
         keep(res, v)
         target4 = shrink3(r)
         v = solve(4, target4)
         for e in range(3):
-            v = relax(4, target4, around(4, 4 + e, v))
+            v = relax(4, target4, around(4, 4 + e, v, chunks))
         w = load(res, 2)
         v = [[w[a][g] + v[0][g] for g in range(8)] for a in range(2)]
-        v = relax(3, target3(), around(3, 7, v))
-        v = relax(3, target3(), around(3, 8, v))
+        v = relax(3, target3(), around(3, 7, v, chunks))
+        v = relax(3, target3(), around(3, 8, v, chunks))
         w = load(rhs2, 2)
         v = [[w[a][g] + v[a][g] for g in range(8)] for a in range(2)]
-        v = relax(2, target2(), around(2, 9, v))
-        v = relax(2, target2(), around(2, 10, v))
+        v = relax(2, target2(), around(2, 9, v, chunks))
+        v = relax(2, target2(), around(2, 10, v, chunks))
         for a in range(2):
             for g in range(8):
                 back_b[g, a] = v[a][g]
 
     nacc[...] = jnp.zeros((CYCLES, 8, 128), F32)
+
+    for both in early:
+        both.wait()
 
     @pl.loop(0, CYCLES)
     def _(cycle):
         this = lax.rem(cycle, 2)
         other = 1 - this
-        sweep0(this, other)
-        exchange0(other)
-        sweep0(other, this)
-        exchange0(this)
+
+        @pl.when(cycle == 0)
+        def _():
+            @pl.loop(0, 8)
+            def _(p):
+                for half in range(2):
+                    for row in range(0, 256, 64):
+                        fresh = j0[p, half, pl.ds(row, 64), :] * g0[p, half, pl.ds(row, 64), :]
+                        vb[2, p + 1, half, pl.ds(PAD + row, 64), :] = fresh
+
+            sweep0(2, 0, 1)
+            late.wait()
+
+        @pl.when(cycle > 0)
+        def _():
+            sweep0(this, 2, 0)
+            exchange0(2, 0)
+            sweep0(2, this, 0)
+            exchange0(this, 1)
+
         residual0(this, True, 0)
-        shrink0(r0, g1)
-
-        @pl.loop(0, 4)
+        shrink0(r0, g1, 4)
+        both = pair(3, (g1.at[6:8], g1.at[2:4]), (g1.at[4:6], g1.at[8:10]))
+        both.start()
+        both.wait()
+
+        @pl.loop(0, 8)
         def _(p):
-            wb[0, p + 1, pl.ds(PAD, 128), :] = j1[p] * g1[p]
-
-        exchange1(0)
-        sweep1(0, store_second)
-        exchange1(1)
+            wb[0, p + 3, pl.ds(PAD, 128), :] = j1[p + 2] * g1[p + 2]
+
+        sweep1(0, store_second, 1)
         residual1()
 
+        chunks = []
+
+        def chunk(up, down, steps=1):
+            i = len(chunks)
+            chunks.append(Pair(up, down, c_send.at[i], c_recv.at[i], steps))
+
+        for i in range(2):
+            chunk((g1.at[4 + i], g1.at[i]), (g1.at[6 + i], g1.at[10 + i]))
+        rows = pl.ds(PAD, 128)
+        chunk((wb.at[1, 8, rows], wb.at[1, 0, rows]), (wb.at[1, 5, rows], wb.at[1, 13, rows]), 2)
+        for i in range(3):
+            chunk(
+                (wb.at[1, 5 + i, rows], wb.at[1, 1 + i, rows]),
+                (wb.at[1, 6 + i, rows], wb.at[1, 10 + i, rows]),
+            )
+        for i in range(2):
+            for half in range(2):
+                for row in range(0, 256, 128):
+                    rows = pl.ds(PAD + row, 128)
+                    chunk(
+                        (vb.at[this, 4 + i, half, rows], vb.at[this, i, half, rows]),
+                        (vb.at[this, 4 + i, half, rows], vb.at[this, 8 + i, half, rows]),
+                    )
+
         send_a[...] = shrink1(r1).reshape(16, 8, 128)
-        all_wide(send_a, snake_wide, recv_a, gz, a_send, a_recv)
+        finish = all_wide(send_a, snake_wide, recv_a, gz, a_send, a_recv)
+        chunks[0].start()
+        chunks[1].start()
+        finish()
         turned = recv_a[...].reshape(128, 128).T
         for a in range(2):
             send_b[:, a] = turned[64 * a : 64 * a + 64].reshape(8, 8, 128)
-        all_narrow(send_b, snake_narrow, recv_b, gy, b_send, b_recv)
-        lines()
-        all_narrow(back_b, lambda g: g, got_b, narrow, bb_send, bb_recv)
+        all_narrow(send_b, snake_narrow, recv_b, gy, b_send, b_recv)()
+        lines(chunks)
+        all_narrow(back_b, lambda g: g, got_b, narrow, bb_send, bb_recv)()
         turned = jnp.concatenate([got_b[:, a].reshape(64, 128) for a in range(2)], axis=0).T
         back_a[...] = turned.reshape(16, 8, 128)
-        all_wide(back_a, lambda g: g, got_a, wide, ba_send, ba_recv)
-
-        @pl.loop(0, 4)
-        def _(p):
-            wb[0, p + 1, pl.ds(PAD, 128), :] = wb[1, p + 1, pl.ds(PAD, 128), :]
-
-        for a in range(2):
-            grown[a] = dot(got_a[...].reshape(128, 128), spread[a])
-        for a in range(2):
-            for b in range(2):
-                for p in range(4):
-                    piece = grown[a, pl.ds(b * 4 + p, 16, 8), :]
+        finish = all_wide(back_a, lambda g: g, got_a.at[1], wide, ba_send, ba_recv)
+        chunks[13].start()
+        finish()
+
+        lhs[0] = got_a[1].reshape(128, 128)
+        ends[0] = lhs[0, pl.ds(3, 32, 4), :]
+        ends[1] = lhs[0, pl.ds(0, 32, 4), :]
+        whole = pair(10, (got_a.at[1], got_a.at[0]), (got_a.at[1], got_a.at[2]))
+        outer = pair(11, (ends.at[0], beyond.at[0]), (ends.at[1], beyond.at[1]), 2)
+        whole.start()
+        outer.start()
+        for each in chunks:
+            each.wait()
+        whole.wait()
+        outer.wait()
+        for side in range(3):
+            for a in range(2):
+                grown[a] = dot(got_a[side].reshape(128, 128), spread[a])
+            for a in range(2):
+                for b in range(2):
+                    for p in range(4):
+                        piece = grown[a, pl.ds(b * 4 + p, 16, 8), :]
+                        for i in range(2):
+                            rows = pl.ds(PAD + 4 * a + 2 * b + i, 16, 8)
+                            q = 4 * side + p + 1
+                            wb[0, q, rows, :] = wb[1, q, rows, :] + piece
+        for side in range(2):
+            for a in range(2):
+                grown[a, 0:32, :] = dot(beyond[side], spread[a])
+                for b in range(2):
+                    piece = grown[a, pl.ds(b, 16, 2), :]
                     for i in range(2):
                         rows = pl.ds(PAD + 4 * a + 2 * b + i, 16, 8)
-                        wb[0, p + 1, rows, :] = wb[0, p + 1, rows, :] + piece
-        exchange1(0)
-        sweep1(0, store_second)
-        exchange1(1)
-        sweep1(1, store_error)
-
-        @pl.loop(0, 4)
+                        wb[0, 13 * side, rows, :] = wb[1, 13 * side, rows, :] + piece
+        sweep1(0, store_second, 4)
+        sweep1(1, store_error, 3)
+
+        @pl.loop(0, 10)
         def _(p):
             for half in range(2):
                 piece = dot(e1[p], spread[half])
                 for i in range(2):
                     rows = pl.ds(PAD + i, 128, 2)
-                    vb[other, p + 1, half, rows, :] = vb[this, p + 1, half, rows, :] + piece
-
-        exchange0(other)
-        sweep0(other, this)
-        exchange0(this)
-        sweep0(this, other)
-        exchange0(other)
+                    vb[other, p, half, rows, :] = vb[this, p, half, rows, :] + piece
+
+        sweep0(other, this, 2)
+        sweep0(this, other, 1)
         residual0(other, False, cycle)
 
     stores = []
@@ -617,7 +750,7 @@
         for half in range(2):
             stores.append(
                 pltpu.make_async_copy(
-                    vb.at[CYCLES % 2, p + 1, half, pl.ds(PAD, 256)],
+                    vb.at[CYCLES % 2, p + 3, half, pl.ds(PAD, 256)],
                     out.at[p, :, pl.ds(half * 128, 128)],
                     in_sem.at[0, p, half],
                 )
@@ -693,19 +826,20 @@
         ],
         out_specs=(pl.BlockSpec(memory_space=pl.ANY), pl.BlockSpec(memory_space=pltpu.SMEM)),
         scratch_shapes=[
-            vmem(2, 6, 2, 256 + 2 * PAD, 128),
+            vmem(3, 10, 2, 256 + 2 * PAD, 128),
+            vmem(8, 2, 256, 128),
             vmem(4, 2, 256, 128),
+            vmem(8, 2, 256, 128),
             vmem(4, 2, 256, 128),
-            vmem(4, 2, 256, 128),
-            vmem(4, 2, 256, 128),
-            vmem(2, 6, 128 + 2 * PAD, 128),
+            vmem(12, 8, 128),
+            vmem(2, 14, 128 + 2 * PAD, 128),
+            vmem(12, 128, 128),
             vmem(4, 128, 128),
+            vmem(12, 128, 128),
             vmem(4, 128, 128),
-            vmem(4, 128, 128),
-            vmem(4, 128, 128),
-            vmem(4, 128, 128),
-            vmem(2, 128, 128),
-            vmem(2, 128, 128),
+            vmem(10, 128, 128),
+            pltpu.VMEM((2, 128, 128), jnp.bfloat16),
+            pltpu.VMEM((2, 128, 128), jnp.bfloat16),
             vmem(2, 128, 128),
             vmem(16, 16, 128),
             vmem(16, 16, 128),
@@ -718,7 +852,9 @@
             vmem(8, 2, 8, 128),
             vmem(8, 2, 8, 128),
             vmem(16, 8, 128),
-            vmem(16, 8, 128),
+            vmem(3, 16, 8, 128),
+            vmem(2, 32, 128),
+            vmem(2, 32, 128),
             vmem(2, 128, 128),
             vmem(5, 64, 128),
             vmem(2, 64, 128),
@@ -734,8 +870,10 @@
             vmem(GROUP_Y, CYCLES, 8, 128),
             vmem(GROUP_Z, CYCLES, 8, 128),
             dma((2, 4, 2)),
-            dma((2, 2, 2)),
-            dma((2, 2, 2)),
+            dma((12, 2)),
+            dma((12, 2)),
+            dma((14, 2)),
+            dma((14, 2)),
             dma((GROUP_Z,)),
             dma((GROUP_Z,)),
             dma((GROUP_Y,)),

time: 316 us -> 294 us (0.930)
  Pallas kernels: 311 us -> 289 us
    pallas_call x1, Pallas kernels: 311 us -> 289 us  [shards(): pl.pallas_call(kernel, out_shape=(jax.ShapeDtypeStruct((4, 256, 256), F32...]
where the time goes in v1:
time: 294 us
  Pallas kernels  289 us (98%)
  local copies, waits for them, and re-layouts  4.58 us (2%)
    pallas_call x1, Pallas kernels, shards(): pl.pallas_call(kernel, out_shape=(jax.ShapeDtypeStruct((4, 256, 256), F32...  289 us

profile of v1, /device:TPU:1, one launch (start us, length us, event | category | flops | bytes accessed | tf_op | source)
XLA Modules:
  0.0 294.1 jit_solution(8718891354856859402)
XLA Ops:
  0.6 0.0 copy-start
  0.6 1.2 copy-done
  1.9 0.0 copy-start.1
  1.9 1.2 copy-done.1
  3.1 0.0 copy-start.2
  3.1 0.7 copy-done.2
  3.7 288.8 %shard_map.50 = (f32[4,256,256]{2,1,0:T(8,128)S(1)}, f32[2]{0:T(128)S(1)}) custom-call(f32[4,256,256]{2,1,0:T(8,128)S(1)} %copy-done, f32[4]{0:T(128)S(1)} %copy-done.2, f32[4,256,256]{2,1,0:T(8,128)S(1)} %copy-done.1), custom_call_target="tpu_custom_call" | custom-call | tf_op jit(solution)/shard_map/pallas_call | solution.py:816
  292.6 1.0 copy.7
  293.6 0.5 copy.8
Async XLA Ops:
  0.6 1.2 copy-start
  1.9 1.2 copy-start.1
  3.1 0.7 copy-start.2

commit v2 on v1

--- a/solution.py
+++ b/solution.py
@@ -20,14 +20,31 @@
 PAD = 8
 
 
-def snake_wide(g):
-    high, quarter, core = lax.div(g, 8), lax.div(lax.rem(g, 8), 2), lax.rem(g, 2)
-    return high * 8 + 2 * (quarter + high * (3 - 2 * quarter)) + core
-
-
-def snake_narrow(g):
-    high, quarter = lax.div(g, 4), lax.rem(g, 4)
-    return high * 4 + quarter + high * (3 - 2 * quarter)
+def device_of(a, b):
+    wide = lax.div(a, 8) * 8 + lax.rem(lax.div(a, 2), 4) * 2 + lax.div(b, 4)
+    return (wide, lax.rem(a, 2) * 4 + lax.rem(b, 4))
+
+
+def place_wide(a):
+    z, x = lax.div(a, 8) * 2 + lax.rem(a, 2), lax.rem(lax.div(a, 2), 4)
+    return z * 4 + x + lax.rem(z, 2) * (3 - 2 * x)
+
+
+def member_wide(place):
+    z, x = lax.div(place, 4), lax.rem(place, 4)
+    x = x + lax.rem(z, 2) * (3 - 2 * x)
+    return (lax.div(z, 2) * 4 + x) * 2 + lax.rem(z, 2)
+
+
+def place_narrow(b):
+    core, y = lax.div(b, 4), lax.rem(b, 4)
+    return y * 2 + core + lax.rem(y, 2) * (1 - 2 * core)
+
+
+def member_narrow(place):
+    y, core = lax.div(place, 2), lax.rem(place, 2)
+    core = core + lax.rem(y, 2) * (1 - 2 * core)
+    return core * 4 + y
 
 
 def dot(a, b):
@@ -58,41 +75,63 @@
 
 
 def below(v, s):
-    if s < 4:
-        inner = lane_iota() % 4 >= s
-        return [
-            jnp.where(inner, roll_lanes(v[g], s), roll_lanes(v[g - 1], s - 4 if g else s + 4))
-            for g in range(8)
-        ]
-    if s < 32:
+    low = lax.div(lax.rem(lane_iota(), 16), 8) == 1
+    result = []
+    for g in range(8):
+        c, y = divmod(g, 4)
         t = s // 4
-        return [v[g - t] if g >= t else roll_lanes(v[g - t + 8], 8) for g in range(8)]
-    return [roll_lanes(v[g], s // 4) for g in range(8)]
+        if s < 4:
+            if y:
+                other = roll_lanes(v[g - 1], s - 4)
+            else:
+                carry = roll_lanes(v[3], s - 12) if c else roll_lanes(v[7], s + 4)
+                other = jnp.where(low, roll_lanes(v[4 * c + 3], s + 4), carry)
+            result.append(jnp.where(lane_iota() % 4 >= s, roll_lanes(v[g], s), other))
+        elif s < 16 and y >= t:
+            result.append(v[g - t])
+        elif s < 32:
+            y = y - t + 4 if s < 16 else y
+            carry = roll_lanes(v[y], -8) if c else roll_lanes(v[4 + y], 8)
+            result.append(jnp.where(low, roll_lanes(v[4 * c + y], 8), carry))
+        elif s == 32:
+            result.append(v[y] if c else roll_lanes(v[4 + y], 16))
+        else:
+            result.append(roll_lanes(v[g], t))
+    return result
 
 
 def above(v, s):
-    if s < 4:
-        inner = lane_iota() % 4 < 4 - s
-        return [
-            jnp.where(
-                inner,
-                roll_lanes(v[g], -s),
-                roll_lanes(v[(g + 1) % 8], 4 - s if g < 7 else -4 - s),
-            )
-            for g in range(8)
-        ]
-    if s < 32:
+    low = lax.div(lax.rem(lane_iota(), 16), 8) == 1
+    result = []
+    for g in range(8):
+        c, y = divmod(g, 4)
         t = s // 4
-        return [v[g + t] if g + t < 8 else roll_lanes(v[g + t - 8], -8) for g in range(8)]
-    return [roll_lanes(v[g], -(s // 4)) for g in range(8)]
+        if s < 4:
+            if y < 3:
+                other = roll_lanes(v[g + 1], 4 - s)
+            else:
+                carry = roll_lanes(v[0], -4 - s) if c else roll_lanes(v[4], 12 - s)
+                other = jnp.where(low, carry, roll_lanes(v[4 * c], -4 - s))
+            result.append(jnp.where(lane_iota() % 4 < 4 - s, roll_lanes(v[g], -s), other))
+        elif s < 16 and y + t < 4:
+            result.append(v[g + t])
+        elif s < 32:
+            y = y + t - 4 if s < 16 else y
+            carry = roll_lanes(v[y], -8) if c else roll_lanes(v[4 + y], 8)
+            result.append(jnp.where(low, carry, roll_lanes(v[4 * c + y], -8)))
+        elif s == 32:
+            result.append(roll_lanes(v[y], -16) if c else v[4 + y])
+        else:
+            result.append(roll_lanes(v[g], -t))
+    return result
 
 
 def kernel(
     source, vertical, reaction, out, norms,
-    vb, g0, d0, j0, r0, vt, wb, g1, d1, j1, r1, e1, compact, spread, lhs,
+    v_a, v_b, v_c, v_d, g0, d0, j0, r0, vt, w_a, w_b, g1, d1, j1, r1, e1, compact, spread, lhs,
     send_as, recv_as, send_bs, recv_bs, send_a, recv_a, send_b, recv_b,
     back_b, got_b, back_a, got_a, beyond, ends, grown,
-    dl, vl, cf, val, hx, hy, ys, rhs2, rhs3, res,
+    dl, vl, cf, val, hx, xs, hy, ys, rhs2, rhs3, res,
     nacc, nb, nz,
     in_sem, z_send, z_recv, c_send, c_recv,
     as_send, as_recv, bs_send, bs_recv, a_send, a_recv, b_send, b_recv,
@@ -100,7 +139,10 @@
 ):
     gz, gy = lax.axis_index("gz"), lax.axis_index("gy")
     me = gz * GROUP_Y + gy
-    wide, narrow = snake_wide(gz), snake_narrow(gy)
+    core = lax.rem(gz, 2)
+    ia = (lax.div(gz, 8) * 4 + lax.div(lax.rem(gz, 8), 2)) * 2 + lax.div(gy, 4)
+    ib = core * 4 + lax.rem(gy, 4)
+    wide, narrow = place_wide(ia), place_narrow(ib)
 
     def device(d):
         d = lax.rem(d + DEVICES, DEVICES)
@@ -115,30 +157,34 @@
     for copy in loads:
         copy.start()
 
-    @pl.loop(0, 30)
+    @pl.loop(0, 10)
     def _(i):
-        for half in range(2):
-            for row in (0, PAD + 256):
-                vb[lax.div(i, 10), lax.rem(i, 10), half, pl.ds(row, PAD), :] = jnp.zeros((PAD, 128), F32)
-
-    @pl.loop(0, 28)
+        for ref in (v_a, v_b, v_c, v_d):
+            for half in range(2):
+                for row in (0, PAD + 256):
+                    ref[i, half, pl.ds(row, PAD), :] = jnp.zeros((PAD, 128), F32)
+
+    @pl.loop(0, 14)
     def _(i):
-        for row in (0, PAD + 128):
-            wb[lax.div(i, 14), lax.rem(i, 14), pl.ds(row, PAD), :] = jnp.zeros((PAD, 128), F32)
+        for ref in (w_a, w_b):
+            for row in (0, PAD + 128):
+                ref[i, pl.ds(row, PAD), :] = jnp.zeros((PAD, 128), F32)
 
     for p in range(4):
         vt[p + 4] = jnp.full((8, 128), vertical[p], F32)
 
     @pl.when(jnp.logical_or(me < 2, me >= DEVICES - 2))
     def _():
-        @pl.loop(0, 30)
+        @pl.loop(0, 10)
         def _(i):
-            for half in range(2):
-                vb[lax.div(i, 10), lax.rem(i, 10), half] = jnp.zeros((256 + 2 * PAD, 128), F32)
-
-        @pl.loop(0, 28)
+            for ref in (v_a, v_b, v_c, v_d):
+                for half in range(2):
+                    ref[i, half] = jnp.zeros((256 + 2 * PAD, 128), F32)
+
+        @pl.loop(0, 14)
         def _(i):
-            wb[lax.div(i, 14), lax.rem(i, 14)] = jnp.zeros((128 + 2 * PAD, 128), F32)
+            for ref in (w_a, w_b):
+                ref[i] = jnp.zeros((128 + 2 * PAD, 128), F32)
 
         for i in (0, 1, 6, 7):
             for half in range(2):
@@ -156,12 +202,12 @@
     @pl.when(wide == 0)
     def _():
         for e in range(EVENTS):
-            hx[e, 0] = jnp.zeros((64, 128), F32)
+            hx[e, 0] = jnp.zeros((32, 128), F32)
 
     @pl.when(wide == GROUP_Z - 1)
     def _():
         for e in range(EVENTS):
-            hx[e, 1] = jnp.zeros((64, 128), F32)
+            hx[e, 1] = jnp.zeros((32, 128), F32)
 
     @pl.when(narrow == 0)
     def _():
@@ -181,22 +227,13 @@
 
     barrier = pltpu.get_barrier_semaphore()
     for k in range(1, GROUP_Z):
-        pl.semaphore_signal(barrier, inc=1, device_id=(lax.rem(gz + k, GROUP_Z), gy), device_id_type=MESH)
+        pl.semaphore_signal(barrier, inc=1, device_id=device_of(lax.rem(ia + k, GROUP_Z), ib), device_id_type=MESH)
     for k in range(1, GROUP_Y):
-        pl.semaphore_signal(barrier, inc=1, device_id=(gz, lax.rem(gy + k, GROUP_Y)), device_id_type=MESH)
-
-    for side, near, far in ((-1, 0, 1), (1, GROUP_Y - 1, GROUP_Y - 2)):
-        for edge, steps in ((near, 1), (near, 2), (far, 2)):
-
-            @pl.when(gy == edge)
-            def _(side=side, steps=steps):
-                pl.semaphore_signal(
-                    barrier, inc=1, device_id=device(me + side * steps), device_id_type=MESH
-                )
-
-    outside = 2 * jnp.logical_or(gy == 0, gy == GROUP_Y - 1).astype(jnp.int32)
-    outside = outside + jnp.logical_or(gy == 1, gy == GROUP_Y - 2).astype(jnp.int32)
-    pl.semaphore_wait(barrier, GROUP_Z + GROUP_Y - 2 + outside)
+        pl.semaphore_signal(barrier, inc=1, device_id=device_of(ia, lax.rem(ib + k, GROUP_Y)), device_id_type=MESH)
+
+    for shift in (-2, -1, 1, 2):
+        pl.semaphore_signal(barrier, inc=1, device_id=device(me + shift), device_id_type=MESH)
+    pl.semaphore_wait(barrier, GROUP_Z + GROUP_Y + 2)
 
     has_up, has_down = me < DEVICES - 1, me > 0
 
@@ -233,8 +270,8 @@
         rows = pl.ds(PAD, 256)
         both = pair(
             i,
-            (vb.at[slot, 6, :, rows], vb.at[slot, 2, :, rows]),
-            (vb.at[slot, 3, :, rows], vb.at[slot, 7, :, rows]),
+            (slot.at[6, :, rows], slot.at[2, :, rows]),
+            (slot.at[3, :, rows], slot.at[7, :, rows]),
         )
         both.start()
         both.wait()
@@ -242,16 +279,16 @@
     def all_wide(src, pick, dst, place, send_sem, recv_sem):
         copies = []
         for k in range(1, GROUP_Z):
-            peer = lax.rem(gz + k, GROUP_Z)
+            peer = lax.rem(ia + k, GROUP_Z)
             copies.append(
                 pltpu.make_async_remote_copy(
                     src_ref=src.at[pick(peer)], dst_ref=dst.at[place], send_sem=send_sem.at[k],
-                    recv_sem=recv_sem.at[k], device_id=(peer, gy), device_id_type=MESH,
+                    recv_sem=recv_sem.at[k], device_id=device_of(peer, ib), device_id_type=MESH,
                 )
             )
         for copy in copies:
             copy.start()
-        dst[place] = src[pick(gz)]
+        dst[place] = src[pick(ia)]
 
         def finish():
             for copy in copies:
@@ -262,16 +299,16 @@
     def all_narrow(src, pick, dst, place, send_sem, recv_sem):
         copies = []
         for k in range(1, GROUP_Y):
-            peer = lax.rem(gy + k, GROUP_Y)
+            peer = lax.rem(ib + k, GROUP_Y)
             copies.append(
                 pltpu.make_async_remote_copy(
                     src_ref=src.at[pick(peer)], dst_ref=dst.at[place], send_sem=send_sem.at[k],
-                    recv_sem=recv_sem.at[k], device_id=(gz, peer), device_id_type=MESH,
+                    recv_sem=recv_sem.at[k], device_id=device_of(ia, peer), device_id_type=MESH,
                 )
             )
         for copy in copies:
             copy.start()
-        dst[place] = src[pick(gy)]
+        dst[place] = src[pick(ib)]
 
         def finish():
             for copy in copies:
@@ -284,7 +321,7 @@
 
     def around0(slot, p, row):
         rows = pl.ds(PAD + row, BLOCK)
-        centre = [vb[slot, p + 3, half, rows, :] for half in range(2)]
+        centre = [slot[p + 3, half, rows, :] for half in range(2)]
         left = [pltpu.roll(c, 1, 1) for c in centre]
         right = [pltpu.roll(c, 127, 1) for c in centre]
         sums = [
@@ -294,9 +331,9 @@
         coupled = jnp.broadcast_to(vt[p + 4, 0:1, :], (BLOCK, 128))
         total = []
         for half in range(2):
-            beside = vb[slot, p + 3, half, pl.ds(PAD + row - 1, BLOCK), :]
-            beside = beside + vb[slot, p + 3, half, pl.ds(PAD + row + 1, BLOCK), :]
-            along = vb[slot, p + 2, half, rows, :] + vb[slot, p + 4, half, rows, :]
+            beside = slot[p + 3, half, pl.ds(PAD + row - 1, BLOCK), :]
+            beside = beside + slot[p + 3, half, pl.ds(PAD + row + 1, BLOCK), :]
+            along = slot[p + 2, half, rows, :] + slot[p + 4, half, rows, :]
             total.append(H[0] * (sums[half] + beside) + coupled * along)
         return centre, total
 
@@ -310,7 +347,7 @@
                 for half in range(2):
                     fresh = g0[p + 2, half, rows, :] + total[half]
                     fresh = (1.0 - OMEGA) * centre[half] + j0[p + 2, half, rows, :] * fresh
-                    vb[new, p + 3, half, pl.ds(PAD + row, BLOCK), :] = fresh
+                    new[p + 3, half, pl.ds(PAD + row, BLOCK), :] = fresh
 
     def residual0(slot, keep, sums):
         @pl.loop(0, 4)
@@ -329,12 +366,12 @@
 
     def around1(slot, p, row):
         rows = pl.ds(PAD + row, BLOCK)
-        centre = wb[slot, p + 5, rows, :]
+        centre = slot[p + 5, rows, :]
         sums = jnp.where(lanes1 == 0, 0.0, pltpu.roll(centre, 1, 1))
         sums = sums + jnp.where(lanes1 == 127, 0.0, pltpu.roll(centre, 127, 1))
-        sums = sums + wb[slot, p + 5, pl.ds(PAD + row - 1, BLOCK), :]
-        sums = sums + wb[slot, p + 5, pl.ds(PAD + row + 1, BLOCK), :]
-        along = wb[slot, p + 4, rows, :] + wb[slot, p + 6, rows, :]
+        sums = sums + slot[p + 5, pl.ds(PAD + row - 1, BLOCK), :]
+        sums = sums + slot[p + 5, pl.ds(PAD + row + 1, BLOCK), :]
+        along = slot[p + 4, rows, :] + slot[p + 6, rows, :]
         return centre, H[1] * sums + jnp.broadcast_to(vt[p + 4, 0:1, :], (BLOCK, 128)) * along
 
     def sweep1(old, store, reach):
@@ -348,7 +385,7 @@
                 store(p, row, (1.0 - OMEGA) * centre + fresh)
 
     def store_second(p, row, fresh):
-        wb[1, p + 5, pl.ds(PAD + row, BLOCK), :] = fresh
+        w_b[p + 5, pl.ds(PAD + row, BLOCK), :] = fresh
 
     def store_error(p, row, fresh):
         e1[p + 3, pl.ds(row, BLOCK), :] = fresh
@@ -357,7 +394,7 @@
         @pl.loop(0, 4)
         def _(p):
             for row in range(0, 128, BLOCK):
-                centre, total = around1(1, p, row)
+                centre, total = around1(w_b, p, row)
                 rows = pl.ds(row, BLOCK)
                 r1[p, rows, :] = g1[p + 4, rows, :] + total - d1[p, rows, :] * centre
 
@@ -419,12 +456,12 @@
         coupling = jnp.where(plane == p, vertical[p], coupling)
     for x in range(16):
         send_as[x, 8:16, :] = coupling
-    all_wide(send_as, snake_wide, recv_as, gz, as_send, as_recv)()
+    all_wide(send_as, place_wide, recv_as, ia, as_send, as_recv)()
     for f in range(2):
         turned = recv_as[:, 8 * f : 8 * f + 8, :].reshape(128, 128).T
         for a in range(2):
             send_bs[:, 2 * f + a] = turned[64 * a : 64 * a + 64].reshape(8, 8, 128)
-    finish = all_narrow(send_bs, snake_narrow, recv_bs, gy, bs_send, bs_recv)
+    finish = all_narrow(send_bs, place_narrow, recv_bs, ib, bs_send, bs_recv)
     early.append(pair(8, (j0.at[4:6], j0.at[0:2]), (j0.at[2:4], j0.at[6:8])))
     late = pair(9, (j1.at[4:8], j1.at[0:4]), (j1.at[4:8], j1.at[8:12]))
     early[-1].start()
@@ -520,11 +557,21 @@
         ys[event, 1, 0:size, :] = val[event, pl.ds(7, size, 8), :]
         span = pl.ds(0, size)
         copies = []
+        for j in range(4):
+            first, last = v[0], v[count - 1]
+            if level == 2:
+                go_down = jnp.where(odd_x, roll_lanes(first[2 * j + 1], 4), first[2 * j])
+                go_up = jnp.where(odd_x, last[2 * j + 1], roll_lanes(last[2 * j], -4))
+            else:
+                go_down = jnp.where(odd_x, first[2 * j + 1], first[2 * j])
+                go_up = jnp.where(odd_x, last[2 * j + 1], last[2 * j])
+            xs[event, 0, tile(j), :] = go_down
+            xs[event, 1, tile(j), :] = go_up
         for side, src, dst, there in (
-            (0, val.at[event, pl.ds(64 * (count - 1), 64)], hx.at[event, 0], (snake_wide(wide + 1), gy)),
-            (1, val.at[event, pl.ds(0, 64)], hx.at[event, 1], (snake_wide(wide - 1), gy)),
-            (2, ys.at[event, 1, span], hy.at[event, 0, span], (gz, snake_narrow(narrow + 1))),
-            (3, ys.at[event, 0, span], hy.at[event, 1, span], (gz, snake_narrow(narrow - 1))),
+            (0, xs.at[event, 1], hx.at[event, 0], device_of(member_wide(wide + 1), ib)),
+            (1, xs.at[event, 0], hx.at[event, 1], device_of(member_wide(wide - 1), ib)),
+            (2, ys.at[event, 1, span], hy.at[event, 0, span], device_of(ia, member_narrow(narrow + 1))),
+            (3, ys.at[event, 0, span], hy.at[event, 1, span], device_of(ia, member_narrow(narrow - 1))),
         ):
             copies.append(
                 pltpu.make_async_remote_copy(
@@ -543,7 +590,16 @@
         for a in range(count):
             mine = []
             for g in range(8):
-                left, right = hx[event, 0, tile(g), :], hx[event, 1, tile(g), :]
+                left, right = hx[event, 0, tile(g // 2), :], hx[event, 1, tile(g // 2), :]
+                if level == 2:
+                    left = left if g % 2 else roll_lanes(left, 4)
+                    right = roll_lanes(right, -4) if g % 2 else right
+                elif g % 2:
+                    left = jnp.where(odd_x, left, roll_lanes(left, -4))
+                    right = jnp.where(odd_x, right, roll_lanes(right, -4))
+                else:
+                    left = jnp.where(odd_x, roll_lanes(left, 4), left)
+                    right = jnp.where(odd_x, roll_lanes(right, 4), right)
                 if level == 2:
                     both = v[0][g] + v[1][g]
                     inner, outer = (both, left + v[0][g]) if a == 0 else (v[1][g] + right, both)
@@ -624,9 +680,6 @@
 
     @pl.loop(0, CYCLES)
     def _(cycle):
-        this = lax.rem(cycle, 2)
-        other = 1 - this
-
         @pl.when(cycle == 0)
         def _():
             @pl.loop(0, 8)
@@ -634,19 +687,19 @@
                 for half in range(2):
                     for row in range(0, 256, 64):
                         fresh = j0[p, half, pl.ds(row, 64), :] * g0[p, half, pl.ds(row, 64), :]
-                        vb[2, p + 1, half, pl.ds(PAD + row, 64), :] = fresh
-
-            sweep0(2, 0, 1)
+                        v_c[p + 1, half, pl.ds(PAD + row, 64), :] = fresh
+
+            sweep0(v_c, v_b, 1)
             late.wait()
 
         @pl.when(cycle > 0)
         def _():
-            sweep0(this, 2, 0)
-            exchange0(2, 0)
-            sweep0(2, this, 0)
-            exchange0(this, 1)
-
-        residual0(this, True, 0)
+            sweep0(v_a, v_d, 0)
+            exchange0(v_d, 0)
+            sweep0(v_d, v_b, 0)
+            exchange0(v_b, 1)
+
+        residual0(v_b, True, 0)
         shrink0(r0, g1, 4)
         both = pair(3, (g1.at[6:8], g1.at[2:4]), (g1.at[4:6], g1.at[8:10]))
         both.start()
@@ -654,9 +707,9 @@
 
         @pl.loop(0, 8)
         def _(p):
-            wb[0, p + 3, pl.ds(PAD, 128), :] = j1[p + 2] * g1[p + 2]
-
-        sweep1(0, store_second, 1)
+            w_a[p + 3, pl.ds(PAD, 128), :] = j1[p + 2] * g1[p + 2]
+
+        sweep1(w_a, store_second, 1)
         residual1()
 
         chunks = []
@@ -668,30 +721,30 @@
         for i in range(2):
             chunk((g1.at[4 + i], g1.at[i]), (g1.at[6 + i], g1.at[10 + i]))
         rows = pl.ds(PAD, 128)
-        chunk((wb.at[1, 8, rows], wb.at[1, 0, rows]), (wb.at[1, 5, rows], wb.at[1, 13, rows]), 2)
+        chunk((w_b.at[8, rows], w_b.at[0, rows]), (w_b.at[5, rows], w_b.at[13, rows]), 2)
         for i in range(3):
             chunk(
-                (wb.at[1, 5 + i, rows], wb.at[1, 1 + i, rows]),
-                (wb.at[1, 6 + i, rows], wb.at[1, 10 + i, rows]),
+                (w_b.at[5 + i, rows], w_b.at[1 + i, rows]),
+                (w_b.at[6 + i, rows], w_b.at[10 + i, rows]),
             )
         for i in range(2):
             for half in range(2):
                 for row in range(0, 256, 128):
                     rows = pl.ds(PAD + row, 128)
                     chunk(
-                        (vb.at[this, 4 + i, half, rows], vb.at[this, i, half, rows]),
-                        (vb.at[this, 4 + i, half, rows], vb.at[this, 8 + i, half, rows]),
+                        (v_b.at[4 + i, half, rows], v_b.at[i, half, rows]),
+                        (v_b.at[4 + i, half, rows], v_b.at[8 + i, half, rows]),
                     )
 
         send_a[...] = shrink1(r1).reshape(16, 8, 128)
-        finish = all_wide(send_a, snake_wide, recv_a, gz, a_send, a_recv)
+        finish = all_wide(send_a, place_wide, recv_a, ia, a_send, a_recv)
         chunks[0].start()
         chunks[1].start()
         finish()
         turned = recv_a[...].reshape(128, 128).T
         for a in range(2):
             send_b[:, a] = turned[64 * a : 64 * a + 64].reshape(8, 8, 128)
-        all_narrow(send_b, snake_narrow, recv_b, gy, b_send, b_recv)()
+        all_narrow(send_b, place_narrow, recv_b, ib, b_send, b_recv)()
         lines(chunks)
         all_narrow(back_b, lambda g: g, got_b, narrow, bb_send, bb_recv)()
         turned = jnp.concatenate([got_b[:, a].reshape(64, 128) for a in range(2)], axis=0).T
@@ -721,7 +774,7 @@
                         for i in range(2):
                             rows = pl.ds(PAD + 4 * a + 2 * b + i, 16, 8)
                             q = 4 * side + p + 1
-                            wb[0, q, rows, :] = wb[1, q, rows, :] + piece
+                            w_a[q, rows, :] = w_b[q, rows, :] + piece
         for side in range(2):
             for a in range(2):
                 grown[a, 0:32, :] = dot(beyond[side], spread[a])
@@ -729,9 +782,9 @@
                     piece = grown[a, pl.ds(b, 16, 2), :]
                     for i in range(2):
                         rows = pl.ds(PAD + 4 * a + 2 * b + i, 16, 8)
-                        wb[0, 13 * side, rows, :] = wb[1, 13 * side, rows, :] + piece
-        sweep1(0, store_second, 4)
-        sweep1(1, store_error, 3)
+                        w_a[13 * side, rows, :] = w_b[13 * side, rows, :] + piece
+        sweep1(w_a, store_second, 4)
+        sweep1(w_b, store_error, 3)
 
         @pl.loop(0, 10)
         def _(p):
@@ -739,18 +792,18 @@
                 piece = dot(e1[p], spread[half])
                 for i in range(2):
                     rows = pl.ds(PAD + i, 128, 2)
-                    vb[other, p, half, rows, :] = vb[this, p, half, rows, :] + piece
-
-        sweep0(other, this, 2)
-        sweep0(this, other, 1)
-        residual0(other, False, cycle)
+                    v_c[p, half, rows, :] = v_b[p, half, rows, :] + piece
+
+        sweep0(v_c, v_b, 2)
+        sweep0(v_b, v_a, 1)
+        residual0(v_a, False, cycle)
 
     stores = []
     for p in range(4):
         for half in range(2):
             stores.append(
                 pltpu.make_async_copy(
-                    vb.at[CYCLES % 2, p + 3, half, pl.ds(PAD, 256)],
+                    v_a.at[p + 3, half, pl.ds(PAD, 256)],
                     out.at[p, :, pl.ds(half * 128, 128)],
                     in_sem.at[0, p, half],
                 )
@@ -758,12 +811,12 @@
     for copy in stores:
         copy.start()
 
-    all_narrow_sum(nacc, nb, gz, gy, n_send, n_recv)
+    all_narrow_sum(nacc, nb, ia, ib, n_send, n_recv)
     total = nb[0]
     for g in range(1, GROUP_Y):
         total = total + nb[g]
     nacc[...] = total
-    all_wide_sum(nacc, nz, gz, gy, n_send, n_recv)
+    all_wide_sum(nacc, nz, ia, ib, n_send, n_recv)
     total = nz[0]
     for g in range(1, GROUP_Z):
         total = total + nz[g]
@@ -773,36 +826,36 @@
         copy.wait()
 
 
-def all_narrow_sum(src, dst, gz, gy, send_sem, recv_sem):
+def all_narrow_sum(src, dst, ia, ib, send_sem, recv_sem):
     copies = []
     for k in range(1, GROUP_Y):
-        peer = lax.rem(gy + k, GROUP_Y)
+        peer = lax.rem(ib + k, GROUP_Y)
         copies.append(
             pltpu.make_async_remote_copy(
-                src_ref=src, dst_ref=dst.at[gy], send_sem=send_sem.at[0, k],
-                recv_sem=recv_sem.at[0, k], device_id=(gz, peer), device_id_type=MESH,
+                src_ref=src, dst_ref=dst.at[ib], send_sem=send_sem.at[0, k],
+                recv_sem=recv_sem.at[0, k], device_id=device_of(ia, peer), device_id_type=MESH,
             )
         )
     for copy in copies:
         copy.start()
-    dst[gy] = src[...]
+    dst[ib] = src[...]
     for copy in copies:
         copy.wait()
 
 
-def all_wide_sum(src, dst, gz, gy, send_sem, recv_sem):
+def all_wide_sum(src, dst, ia, ib, send_sem, recv_sem):
     copies = []
     for k in range(1, GROUP_Z):
-        peer = lax.rem(gz + k, GROUP_Z)
+        peer = lax.rem(ia + k, GROUP_Z)
         copies.append(
             pltpu.make_async_remote_copy(
-                src_ref=src, dst_ref=dst.at[gz], send_sem=send_sem.at[1, k],
-                recv_sem=recv_sem.at[1, k], device_id=(peer, gy), device_id_type=MESH,
+                src_ref=src, dst_ref=dst.at[ia], send_sem=send_sem.at[1, k],
+                recv_sem=recv_sem.at[1, k], device_id=device_of(peer, ib), device_id_type=MESH,
             )
         )
     for copy in copies:
         copy.start()
-    dst[gz] = src[...]
+    dst[ia] = src[...]
     for copy in copies:
         copy.wait()
 
@@ -826,13 +879,17 @@
         ],
         out_specs=(pl.BlockSpec(memory_space=pl.ANY), pl.BlockSpec(memory_space=pltpu.SMEM)),
         scratch_shapes=[
-            vmem(3, 10, 2, 256 + 2 * PAD, 128),
+            vmem(10, 2, 256 + 2 * PAD, 128),
+            vmem(10, 2, 256 + 2 * PAD, 128),
+            vmem(10, 2, 256 + 2 * PAD, 128),
+            vmem(10, 2, 256 + 2 * PAD, 128),
             vmem(8, 2, 256, 128),
             vmem(4, 2, 256, 128),
             vmem(8, 2, 256, 128),
             vmem(4, 2, 256, 128),
             vmem(12, 8, 128),
-            vmem(2, 14, 128 + 2 * PAD, 128),
+            vmem(14, 128 + 2 * PAD, 128),
+            vmem(14, 128 + 2 * PAD, 128),
             vmem(12, 128, 128),
             vmem(4, 128, 128),
             vmem(12, 128, 128),
@@ -860,7 +917,8 @@
             vmem(2, 64, 128),
             vmem(5, 2 * STEPS + 1, 64, 128),
             vmem(EVENTS, 128, 128),
-            vmem(EVENTS, 2, 64, 128),
+            vmem(EVENTS, 2, 32, 128),
+            vmem(EVENTS, 2, 32, 128),
             vmem(EVENTS, 2, 16, 128),
             vmem(EVENTS, 2, 16, 128),
             vmem(2, 64, 128),

time: 294 us -> 244 us (0.83)
  Pallas kernels: 289 us -> 238 us
    pallas_call x1, Pallas kernels: 289 us -> 238 us  [shards(): pl.pallas_call(kernel, out_shape=(jax.ShapeDtypeStruct((4, 256, 256), F32...]
where the time goes in v2:
time: 244 us
  Pallas kernels  238 us (98%)
  local copies, waits for them, and re-layouts  4.58 us (2%)
    pallas_call x1, Pallas kernels, shards(): pl.pallas_call(kernel, out_shape=(jax.ShapeDtypeStruct((4, 256, 256), F32...  238 us

profile of v2, /device:TPU:1, one launch (start us, length us, event | category | flops | bytes accessed | tf_op | source)
XLA Modules:
  0.0 243.6 jit_solution(13378199239772870231)
XLA Ops:
  0.6 0.0 copy-start
  0.6 1.2 copy-done
  1.9 0.0 copy-start.1
  1.9 1.2 copy-done.1
  3.1 0.0 copy-start.2
  3.1 0.7 copy-done.2
  3.7 238.4 %shard_map.50 = (f32[4,256,256]{2,1,0:T(8,128)S(1)}, f32[2]{0:T(128)S(1)}) custom-call(f32[4,256,256]{2,1,0:T(8,128)S(1)} %copy-done, f32[4]{0:T(128)S(1)} %copy-done.2, f32[4,256,256]{2,1,0:T(8,128)S(1)} %copy-done.1), custom_call_target="tpu_custom_call" | custom-call | tf_op jit(solution)/shard_map/pallas_call | solution.py:869
  242.1 1.0 copy.7
  243.1 0.5 copy.8
Async XLA Ops:
  0.6 1.2 copy-start
  1.9 1.2 copy-start.1
  3.1 0.7 copy-start.2

commit v3 on v2

v3 whole, which is shorter than its diff:
```python
import functools

import jax
import jax.numpy as jnp
from jax import lax
from jax.experimental import pallas as pl
from jax.experimental.pallas import tpu as pltpu
from jax.sharding import PartitionSpec as P

F32 = jnp.float32
MESH = pl.DeviceIdType.MESH
CYCLES = 2
STEPS = 9
EVENTS = 11
OMEGA = 0.8
H = (1.0, 0.25, 1.0 / 16, 1.0 / 64, 1.0 / 256)
GROUP_Z = 16
GROUP_Y = 8
DEVICES = 128
PAD = 8


def device_of(a, b):
    wide = lax.div(a, 8) * 8 + lax.rem(lax.div(a, 2), 4) * 2 + lax.div(b, 4)
    return (wide, lax.rem(a, 2) * 4 + lax.rem(b, 4))


def place_wide(a):
    z, x = lax.div(a, 8) * 2 + lax.rem(a, 2), lax.rem(lax.div(a, 2), 4)
    return z * 4 + x + lax.rem(z, 2) * (3 - 2 * x)


def member_wide(place):
    z, x = lax.div(place, 4), lax.rem(place, 4)
    x = x + lax.rem(z, 2) * (3 - 2 * x)
    return (lax.div(z, 2) * 4 + x) * 2 + lax.rem(z, 2)


def place_narrow(b):
    core, y = lax.div(b, 4), lax.rem(b, 4)
    return y * 2 + core + lax.rem(y, 2) * (1 - 2 * core)


def member_narrow(place):
    y, core = lax.div(place, 2), lax.rem(place, 2)
    core = core + lax.rem(y, 2) * (1 - 2 * core)
    return core * 4 + y


def dot(a, b):
    total = None
    for part in range(3):
        piece = a.astype(jnp.bfloat16)
        product = jnp.dot(piece, b, preferred_element_type=F32)
        total = product if total is None else total + product
        if part < 2:
            a = a - piece.astype(F32)
    return total


def roll_lanes(v, s):
    return pltpu.roll(v, s % 128, 1)


def roll_rows(v, s):
    return pltpu.roll(v, s % 8, 0)


def lane_iota():
    return lax.broadcasted_iota(jnp.int32, (8, 128), 1)


def row_iota():
    return lax.broadcasted_iota(jnp.int32, (8, 128), 0)


def below(v, s):
    if s < 4:
        return [v[p - s] if p >= s else roll_lanes(v[p - s + 4], 1) for p in range(4)]
    return [roll_lanes(v[p], s // 4) for p in range(4)]


def above(v, s):
    if s < 4:
        return [v[p + s] if p + s < 4 else roll_lanes(v[p + s - 4], -1) for p in range(4)]
    return [roll_lanes(v[p], -(s // 4)) for p in range(4)]


def exchange_parts(v):
    row, lane = row_iota(), lane_iota()
    for m in (1, 2, 4):
        down = lax.rem(lax.div(row, m), 2)
        across = lax.rem(lax.div(lane, 16 * m), 2)
        moved = jnp.where(
            down == 1,
            roll_rows(roll_lanes(v, -16 * m), m),
            roll_rows(roll_lanes(v, 16 * m), -m),
        )
        v = jnp.where(down == across, v, moved)
    return v


def tile_of(x):
    z, q = divmod(x, 4)
    return ((z // 2) * 4 + (3 - q if z % 2 else q)) * 2 + z % 2


def kernel(
    source, vertical, reaction, out, norms,
    v_a, v_b, v_c, v_d, g0, d0, j0, r0, vt, w_a, w_b, g1, d1, j1, r1, e1, compact, spread, lhs,
    fold, unfold, send_s, recv_s, send_r, recv_r, turn, back_r, got_r, got_a, beyond, ends, grown,
    dl, vl, cf, val, hx, hy, ys, rhs2, rhs3, res,
    nacc, part, nz,
    in_sem, z_send, z_recv, c_send, c_recv,
    all_send, all_recv, h_send, h_recv,
):
    gz, gy = lax.axis_index("gz"), lax.axis_index("gy")
    me = gz * GROUP_Y + gy
    core = lax.rem(gz, 2)
    ia = (lax.div(gz, 8) * 4 + lax.div(lax.rem(gz, 8), 2)) * 2 + lax.div(gy, 4)
    ib = core * 4 + lax.rem(gy, 4)
    wide, narrow = place_wide(ia), place_narrow(ib)

    def device(d):
        d = lax.rem(d + DEVICES, DEVICES)
        return (lax.div(d, GROUP_Y), lax.rem(d, GROUP_Y))

    loads = []
    for p in range(4):
        for half in range(2):
            lanes = pl.ds(half * 128, 128)
            loads.append(pltpu.make_async_copy(source.at[p, :, lanes], g0.at[p + 2, half], in_sem.at[0, p, half]))
            loads.append(pltpu.make_async_copy(reaction.at[p, :, lanes], r0.at[p, half], in_sem.at[1, p, half]))
    for copy in loads:
        copy.start()

    barrier = pltpu.get_barrier_semaphore()

    members = [lax.rem(ib + j, GROUP_Y) for j in range(GROUP_Y)]
    members = [(b, lax.div(b, 4), lax.rem(b, 4)) for b in members]

    def everyone(act):
        def some(k, start):
            a = lax.rem(ia + k, GROUP_Z)
            wide_a, narrow_a = lax.div(a, 2) * 2, lax.rem(a, 2) * 4
            for b, core_b, y_b in members[start:]:
                to = (wide_a + core_b, narrow_a + y_b)
                act(a * GROUP_Y + b, to[0] * GROUP_Y + to[1], to)

        some(0, 1)
        pl.loop(1, GROUP_Z)(lambda k: some(k, 0))

    everyone(
        lambda block, plane, to: pl.semaphore_signal(
            barrier, inc=1, device_id=to, device_id_type=MESH
        )
    )

    for p in range(4):
        vt[p + 4] = jnp.full((8, 128), vertical[p], F32)

    @pl.loop(0, 10)
    def _(i):
        for ref in (v_a, v_b, v_c, v_d):
            for half in range(2):
                for row in (0, PAD + 256):
                    ref[i, half, pl.ds(row, PAD), :] = jnp.zeros((PAD, 128), F32)

    @pl.loop(0, 14)
    def _(i):
        for ref in (w_a, w_b):
            for row in (0, PAD + 128):
                ref[i, pl.ds(row, PAD), :] = jnp.zeros((PAD, 128), F32)

    def clear(side):
        @pl.loop(7 * side, 7 * side + 3)
        def _(i):
            for ref in (v_a, v_b, v_c, v_d):
                for half in range(2):
                    ref[i, half] = jnp.zeros((256 + 2 * PAD, 128), F32)

        @pl.loop(9 * side, 9 * side + 5)
        def _(i):
            for ref in (w_a, w_b):
                ref[i] = jnp.zeros((128 + 2 * PAD, 128), F32)

        for i in range(6 * side, 6 * side + 2):
            for half in range(2):
                g0[i, half] = jnp.zeros((256, 128), F32)
                j0[i, half] = jnp.zeros((256, 128), F32)
        for i in range(8 * side, 8 * side + 4):
            vt[i] = jnp.zeros((8, 128), F32)
            g1[i] = jnp.zeros((128, 128), F32)
            j1[i] = jnp.zeros((128, 128), F32)
        got_a[2 * side] = jnp.zeros((128, 128), F32)
        beyond[side] = jnp.zeros((32, 128), F32)

    for side in range(2):

        @pl.when(me == (DEVICES - 1) * side)
        def _(side=side):
            clear(side)

        @pl.when(me == 1 + (DEVICES - 3) * side)
        def _(side=side):
            for ref in (w_a, w_b):
                ref[13 * side] = jnp.zeros((128 + 2 * PAD, 128), F32)
            beyond[side] = jnp.zeros((32, 128), F32)

    @pl.when(wide == 0)
    def _():
        for e in range(EVENTS):
            hx[e, 0] = jnp.zeros((32, 128), F32)

    @pl.when(wide == GROUP_Z - 1)
    def _():
        for e in range(EVENTS):
            hx[e, 1] = jnp.zeros((32, 128), F32)

    @pl.when(narrow == 0)
    def _():
        for e in range(EVENTS):
            hy[e, 0] = jnp.zeros((16, 128), F32)

    @pl.when(narrow == GROUP_Y - 1)
    def _():
        for e in range(EVENTS):
            hy[e, 1] = jnp.zeros((16, 128), F32)

    from_lane = lax.broadcasted_iota(jnp.int32, (128, 128), 0)
    to_lane = lax.broadcasted_iota(jnp.int32, (128, 128), 1)
    for half in range(2):
        compact[half] = jnp.where(to_lane == 64 * half + from_lane // 2, 0.25, 0.0).astype(jnp.bfloat16)
        part_of = place_narrow(to_lane // 16) * 8 + to_lane % 8
        hit = jnp.logical_and(part_of == from_lane // 2, to_lane // 8 % 2 == half)
        fold[half] = jnp.where(hit, 0.25, 0.0).astype(jnp.bfloat16)
        part_of = place_narrow(from_lane // 16) * 8 + from_lane % 8
        hit = jnp.logical_and(part_of == to_lane // 2, from_lane // 8 % 2 == half)
        unfold[half] = jnp.where(hit, 1.0, 0.0).astype(jnp.bfloat16)
        spread[half] = jnp.where(from_lane == 64 * half + to_lane // 2, 1.0, 0.0).astype(jnp.bfloat16)

    pl.semaphore_wait(barrier, DEVICES - 1)

    has_up, has_down = me < DEVICES - 1, me > 0

    class Pair:
        def __init__(self, up, down, send_sem, recv_sem, steps=1):
            self.steps = steps
            self.copies = [
                pltpu.make_async_remote_copy(
                    src_ref=src, dst_ref=dst, send_sem=send_sem.at[i], recv_sem=recv_sem.at[i],
                    device_id=device(me + shift), device_id_type=MESH,
                )
                for i, (src, dst), shift in ((0, up, steps), (1, down, -steps))
            ]

        def start(self):
            pl.when(me < DEVICES - self.steps)(self.copies[0].start)
            pl.when(me >= self.steps)(self.copies[1].start)

        def wait(self):
            @pl.when(me < DEVICES - self.steps)
            def _():
                self.copies[0].wait_send()
                self.copies[1].wait_recv()

            @pl.when(me >= self.steps)
            def _():
                self.copies[1].wait_send()
                self.copies[0].wait_recv()

    def pair(i, up, down, steps=1):
        return Pair(up, down, z_send.at[i], z_recv.at[i], steps)

    def exchange0(slot, i):
        rows = pl.ds(PAD, 256)
        both = pair(
            i,
            (slot.at[6, :, rows], slot.at[2, :, rows]),
            (slot.at[3, :, rows], slot.at[7, :, rows]),
        )
        both.start()
        return both.wait

    mine = ia * GROUP_Y + ib

    def all_rows(i, src, to_blocks, dst):
        place = me if to_blocks else mine

        def send(block, plane, to):
            pltpu.make_async_remote_copy(
                src_ref=src.at[:, pl.ds(block if to_blocks else plane, 1)],
                dst_ref=dst.at[:, pl.ds(place, 1)],
                send_sem=all_send.at[i], recv_sem=all_recv.at[i], device_id=to,
                device_id_type=MESH,
            ).start()

        everyone(send)
        dst[:, pl.ds(place, 1), :] = src[:, pl.ds(mine if to_blocks else me, 1), :]

        def finish():
            others = pl.ds(0, DEVICES - 1)
            for sem in (all_recv, all_send):
                pltpu.make_async_copy(src.at[:, others], dst.at[:, others], sem.at[i]).wait()

        return finish

    BLOCK = 32
    lanes0 = lax.broadcasted_iota(jnp.int32, (BLOCK, 128), 1)

    def around0(slot, p, row):
        rows = pl.ds(PAD + row, BLOCK)
        centre = [slot[p + 3, half, rows, :] for half in range(2)]
        left = [pltpu.roll(c, 1, 1) for c in centre]
        right = [pltpu.roll(c, 127, 1) for c in centre]
        sums = [
            jnp.where(lanes0 == 0, 0.0, left[0]) + jnp.where(lanes0 == 127, right[1], right[0]),
            jnp.where(lanes0 == 0, left[0], left[1]) + jnp.where(lanes0 == 127, 0.0, right[1]),
        ]
        coupled = jnp.broadcast_to(vt[p + 4, 0:1, :], (BLOCK, 128))
        total = []
        for half in range(2):
            beside = slot[p + 3, half, pl.ds(PAD + row - 1, BLOCK), :]
            beside = beside + slot[p + 3, half, pl.ds(PAD + row + 1, BLOCK), :]
            along = slot[p + 2, half, rows, :] + slot[p + 4, half, rows, :]
            total.append(H[0] * (sums[half] + beside) + coupled * along)
        return centre, total

    def sweep0(old, new, first, count, step=1):
        @pl.loop(0, count)
        def _(i):
            p = first + i * step
            for row in range(0, 256, BLOCK):
                centre, total = around0(old, p, row)
                rows = pl.ds(row, BLOCK)
                for half in range(2):
                    fresh = g0[p + 2, half, rows, :] + total[half]
                    fresh = (1.0 - OMEGA) * centre[half] + j0[p + 2, half, rows, :] * fresh
                    new[p + 3, half, pl.ds(PAD + row, BLOCK), :] = fresh

    def residual0(slot, keep, sums, first, count, step=1):
        @pl.loop(0, count)
        def _(i):
            p = first + i * step
            for row in range(0, 256, BLOCK):
                centre, total = around0(slot, p, row)
                rows = pl.ds(row, BLOCK)
                for half in range(2):
                    left = g0[p + 2, half, rows, :] + total[half] - d0[p, half, rows, :] * centre[half]
                    if keep:
                        r0[p, half, rows, :] = left
                    else:
                        nacc[sums] += (left * left).reshape(BLOCK // 8, 8, 128).sum(axis=0)

    lanes1 = lax.broadcasted_iota(jnp.int32, (BLOCK, 128), 1)

    def around1(slot, p, row):
        rows = pl.ds(PAD + row, BLOCK)
        centre = slot[p + 5, rows, :]
        sums = jnp.where(lanes1 == 0, 0.0, pltpu.roll(centre, 1, 1))
        sums = sums + jnp.where(lanes1 == 127, 0.0, pltpu.roll(centre, 127, 1))
        sums = sums + slot[p + 5, pl.ds(PAD + row - 1, BLOCK), :]
        sums = sums + slot[p + 5, pl.ds(PAD + row + 1, BLOCK), :]
        along = slot[p + 4, rows, :] + slot[p + 6, rows, :]
        return centre, H[1] * sums + jnp.broadcast_to(vt[p + 4, 0:1, :], (BLOCK, 128)) * along

    def sweep1(old, store, reach):
        @pl.loop(0, 4 + 2 * reach)
        def _(i):
            p = i - reach
            for row in range(0, 128, BLOCK):
                centre, total = around1(old, p, row)
                rows = pl.ds(row, BLOCK)
                fresh = j1[p + 4, rows, :] * (g1[p + 4, rows, :] + total)
                store(p, row, (1.0 - OMEGA) * centre + fresh)

    def store_second(p, row, fresh):
        w_b[p + 5, pl.ds(PAD + row, BLOCK), :] = fresh

    def store_error(p, row, fresh):
        e1[p + 3, pl.ds(row, BLOCK), :] = fresh

    def residual1():
        @pl.loop(0, 4)
        def _(p):
            for row in range(0, 128, BLOCK):
                centre, total = around1(w_b, p, row)
                rows = pl.ds(row, BLOCK)
                r1[p, rows, :] = g1[p + 4, rows, :] + total - d1[p, rows, :] * centre

    def shrink0(src, dst, first):
        @pl.loop(0, 4)
        def _(p):
            total = jnp.zeros((128, 128), F32)
            for half in range(2):
                pairs = src[p, half, pl.ds(0, 128, 2), :] + src[p, half, pl.ds(1, 128, 2), :]
                total = total + dot(pairs, compact[half])
            dst[p + first] = total

    def shrink1(src):
        total = jnp.zeros((128, 128), F32)
        for a in range(2):
            for b in range(2):
                for p in range(4):
                    first = 4 * a + 2 * b
                    pairs = src[p, pl.ds(first, 16, 8), :] + src[p, pl.ds(first + 1, 16, 8), :]
                    lhs[a, pl.ds(b * 4 + p, 16, 8), :] = pairs
            total = total + dot(lhs[a], fold[a])
        return total

    early = []
    for i in range(2):
        for half in range(2):
            lanes = pl.ds(half * 128, 128)
            early.append(
                pair(
                    4 + 2 * i + half,
                    (source.at[2 + i, :, lanes], g0.at[i, half]),
                    (source.at[i, :, lanes], g0.at[6 + i, half]),
                )
            )
    early.append(pair(2, (vt.at[4:8], vt.at[0:4]), (vt.at[4:8], vt.at[8:12])))
    for both in early:
        both.start()
    for copy in loads:
        copy.wait()
    shrink0(r0, r1, 0)

    @pl.loop(0, 4)
    def _(p):
        coupled = 2.0 * vertical[p]
        for half in range(2):
            for row in range(0, 256, 64):
                rows = pl.ds(row, 64)
                diagonal = coupled + 4.0 * H[0] + r0[p, half, rows, :]
                d0[p, half, rows, :] = diagonal
                j0[p + 2, half, rows, :] = OMEGA / diagonal
        diagonal = coupled + 4.0 * H[1] + r1[p]
        d1[p] = diagonal
        j1[p + 4] = OMEGA / diagonal

    def send_blocks(f, v, dst):
        for x in range(16):
            dst[f, 8 * tile_of(x) : 8 * tile_of(x) + 8, :] = exchange_parts(v[8 * x : 8 * x + 8])

    send_blocks(0, shrink1(r1), send_s)
    plane = lane_iota() // 16 % 4
    coupling = jnp.zeros((8, 128), F32)
    for p in range(4):
        coupling = jnp.where(plane == p, vertical[p], coupling)
    for x in range(16):
        send_s[1, 8 * x : 8 * x + 8, :] = coupling
    finish = all_rows(0, send_s, True, recv_s)
    early.append(pair(8, (j0.at[4:6], j0.at[0:2]), (j0.at[2:4], j0.at[6:8])))
    late = pair(9, (j1.at[6:8], j1.at[2:4]), (j1.at[4:6], j1.at[8:10]))
    later = pair(12, (j1.at[4:6], j1.at[0:2]), (j1.at[6:8], j1.at[10:12]))
    early[-1].start()
    late.start()
    finish()

    lane, row = lane_iota(), row_iota()

    def tile(p):
        return pl.ds(8 * p, 8)

    def unpack(v):
        return [
            [v[8 * (8 * b + 2 * p + a) : 8 * (8 * b + 2 * p + a) + 8] for p in range(4)]
            for a in range(2)
            for b in range(2)
        ]

    def shrink2(v):
        result = []
        for a in range(2):
            mine = []
            for p in range(4):
                t = v[2 * a][p] + v[2 * a + 1][p]
                t = t + jnp.where(row % 2 == 1, roll_rows(t, 1), roll_rows(t, -1))
                mine.append(0.25 * t)
            result.append(mine)
        return result

    def shrink3(v):
        mine = []
        for p in range(4):
            t = v[0][p] + v[1][p]
            t = t + jnp.where(row % 4 >= 2, roll_rows(t, 2), roll_rows(t, -2))
            mine.append(0.25 * t)
        return [mine]

    couplings = unpack(recv_s[1].T)[0]
    for p in range(4):
        vl[0, tile(p), :] = jnp.where(lane == 0, 0.0, couplings[p]) if p == 0 else couplings[p]
        vl[1, tile(p), :] = jnp.where(lane == 127, 0.0, couplings[p]) if p == 3 else couplings[p]
    react2 = unpack(recv_s[0].T)
    react3 = shrink2(react2)
    react4 = shrink3(react3)
    order = [(2, each) for each in react2] + [(3, each) for each in react3] + [(4, react4[0])]
    for i, (level, lines) in enumerate(order):
        for p in range(4):
            dl[i, tile(p), :] = 2.0 * couplings[p] + 4.0 * H[level] + lines[p]

    @pl.loop(0, 7)
    def _(i):
        low = [-vl[0, tile(g), :] for g in range(4)]
        high = [-vl[1, tile(g), :] for g in range(4)]
        middle = [dl[i, tile(g), :] for g in range(4)]
        for k in range(STEPS):
            s = 1 << k
            middle_below, middle_above = below(middle, s), above(middle, s)
            left = [-low[g] / middle_below[g] for g in range(4)]
            right = [-high[g] / middle_above[g] for g in range(4)]
            for g in range(4):
                cf[i, 2 * k, tile(g), :] = left[g]
                cf[i, 2 * k + 1, tile(g), :] = right[g]
            high_below, low_above = below(high, s), above(low, s)
            middle = [middle[g] + left[g] * high_below[g] + right[g] * low_above[g] for g in range(4)]
            if k < STEPS - 1:
                low_below, high_above = below(low, s), above(high, s)
                low = [left[g] * low_below[g] for g in range(4)]
                high = [right[g] * high_above[g] for g in range(4)]
        for g in range(4):
            cf[i, 2 * STEPS, tile(g), :] = 1.0 / middle[g]

    first_of = {2: 0, 3: 4, 4: 6}
    count_of = {2: 4, 3: 2, 4: 1}

    def solve(level, right):
        solved = []
        for a in range(count_of[level]):
            i = first_of[level] + a
            r = right[a]
            for k in range(STEPS):
                s = 1 << k
                down, up = below(r, s), above(r, s)
                r = [
                    r[g] + cf[i, 2 * k, tile(g), :] * down[g] + cf[i, 2 * k + 1, tile(g), :] * up[g]
                    for g in range(4)
                ]
            solved.append([r[g] * cf[i, 2 * STEPS, tile(g), :] for g in range(4)])
        return solved

    def around(level, event, v, chunks):
        count = count_of[level]
        for x in range(count):
            for p in range(4):
                val[event, pl.ds((x * 4 + p) * 8, 8), :] = v[x][p]
        size = 4 * count
        ys[event, 0, 0:size, :] = val[event, pl.ds(0, size, 8), :]
        ys[event, 1, 0:size, :] = val[event, pl.ds(7, size, 8), :]
        span = pl.ds(0, size)
        copies = []
        for side, src, dst, there in (
            (0, val.at[event, pl.ds(32 * (count - 1), 32)], hx.at[event, 0], device_of(member_wide(wide + 1), ib)),
            (1, val.at[event, pl.ds(0, 32)], hx.at[event, 1], device_of(member_wide(wide - 1), ib)),
            (2, ys.at[event, 1, span], hy.at[event, 0, span], device_of(ia, member_narrow(narrow + 1))),
            (3, ys.at[event, 0, span], hy.at[event, 1, span], device_of(ia, member_narrow(narrow - 1))),
        ):
            copies.append(
                pltpu.make_async_remote_copy(
                    src_ref=src, dst_ref=dst, send_sem=h_send.at[event, side],
                    recv_sem=h_recv.at[event, side], device_id=there, device_id_type=MESH,
                )
            )
        has = (wide < GROUP_Z - 1, wide > 0, narrow < GROUP_Y - 1, narrow > 0)
        for side in range(4):
            pl.when(has[side])(copies[side].start)
        chunks[event + 2].start()
        for side in range(4):
            pl.when(has[side])(copies[side].wait_send)
            pl.when(has[side])(copies[side ^ 1].wait_recv)
        shift = 1 << (level - 2)
        result = []
        for x in range(count):
            mine = []
            for p in range(4):
                total = v[x - 1][p] if x else hx[event, 0, tile(p), :]
                total = total + (v[x + 1][p] if x + 1 < count else hx[event, 1, tile(p), :])
                low = jnp.broadcast_to(hy[event, 0, pl.ds(x * 4 + p, 1), :], (8, 128))
                high = jnp.broadcast_to(hy[event, 1, pl.ds(x * 4 + p, 1), :], (8, 128))
                total = total + jnp.where(row < shift, low, roll_rows(v[x][p], shift))
                total = total + jnp.where(row >= 8 - shift, high, roll_rows(v[x][p], -shift))
                mine.append(total)
            result.append(mine)
        return result

    def relax(level, target, total):
        return solve(
            level,
            [
                [target[a][g] + H[level] * total[a][g] for g in range(4)]
                for a in range(count_of[level])
            ],
        )

    def residual(level, target, v, total):
        result = []
        for a in range(count_of[level]):
            down, up = below(v[a], 1), above(v[a], 1)
            result.append([
                target[a][g] + H[level] * total[a][g] - dl[first_of[level] + a, tile(g), :] * v[a][g]
                + vl[0, tile(g), :] * down[g] + vl[1, tile(g), :] * up[g]
                for g in range(4)
            ])
        return result

    def load(ref, count):
        return [[ref[a, tile(g), :] for g in range(4)] for a in range(count)]

    def keep(ref, v):
        for a in range(len(v)):
            for g in range(4):
                ref[a, tile(g), :] = v[a][g]

    def lines(chunks):
        target2 = lambda: unpack(turn)
        v = solve(2, target2())
        v = relax(2, target2(), around(2, 0, v, chunks))
        r = residual(2, target2(), v, around(2, 1, v, chunks))
        keep(rhs2, v)
        keep(rhs3, shrink2(r))
        target3 = lambda: load(rhs3, 2)
        v = solve(3, target3())
        v = relax(3, target3(), around(3, 2, v, chunks))
        r = residual(3, target3(), v, around(3, 3, v, chunks))
        keep(res, v)
        target4 = shrink3(r)
        v = solve(4, target4)
        for e in range(3):
            v = relax(4, target4, around(4, 4 + e, v, chunks))
        w = load(res, 2)
        v = [[w[a][g] + v[0][g] for g in range(4)] for a in range(2)]
        v = relax(3, target3(), around(3, 7, v, chunks))
        v = relax(3, target3(), around(3, 8, v, chunks))
        w = load(rhs2, 4)
        v = [[w[x][p] + v[x // 2][p] for p in range(4)] for x in range(4)]
        v = relax(2, target2(), around(2, 9, v, chunks))
        v = relax(2, target2(), around(2, 10, v, chunks))
        for a in range(2):
            for b in range(2):
                for p in range(4):
                    turn[pl.ds(8 * (8 * b + 2 * p + a), 8), :] = v[2 * a + b][p]

    nacc[...] = jnp.zeros((CYCLES, 8, 128), F32)

    for both in early:
        both.wait()

    @pl.loop(0, CYCLES)
    def _(cycle):
        @pl.when(cycle == 0)
        def _():
            @pl.loop(0, 8)
            def _(p):
                for half in range(2):
                    for row in range(0, 256, 64):
                        fresh = j0[p, half, pl.ds(row, 64), :] * g0[p, half, pl.ds(row, 64), :]
                        v_c[p + 1, half, pl.ds(PAD + row, 64), :] = fresh

            sweep0(v_c, v_b, -1, 6)
            residual0(v_b, True, 0, 1, 2)
            late.wait()

        @pl.when(cycle > 0)
        def _():
            sweep0(v_a, v_d, 0, 2, 3)
            finish = exchange0(v_d, 0)
            sweep0(v_a, v_d, 1, 2)
            sweep0(v_d, v_b, 1, 2)
            finish()
            sweep0(v_d, v_b, 0, 2, 3)
            finish = exchange0(v_b, 1)
            residual0(v_b, True, 0, 1, 2)
            finish()

        residual0(v_b, True, 0, 0, 2, 3)
        shrink0(r0, g1, 4)
        both = pair(3, (g1.at[6:8], g1.at[2:4]), (g1.at[4:6], g1.at[8:10]))
        both.start()
        both.wait()

        @pl.loop(0, 8)
        def _(p):
            w_a[p + 3, pl.ds(PAD, 128), :] = j1[p + 2] * g1[p + 2]

        sweep1(w_a, store_second, 1)
        residual1()

        chunks = []

        def chunk(up, down, steps=1):
            i = len(chunks)
            chunks.append(Pair(up, down, c_send.at[i], c_recv.at[i], steps))

        for i in range(2):
            chunk((g1.at[4 + i], g1.at[i]), (g1.at[6 + i], g1.at[10 + i]))
        rows = pl.ds(PAD, 128)
        chunk((w_b.at[8, rows], w_b.at[0, rows]), (w_b.at[5, rows], w_b.at[13, rows]), 2)
        for i in range(3):
            chunk(
                (w_b.at[5 + i, rows], w_b.at[1 + i, rows]),
                (w_b.at[6 + i, rows], w_b.at[10 + i, rows]),
            )
        for i in range(2):
            for half in range(2):
                for row in range(0, 256, 128):
                    rows = pl.ds(PAD + row, 128)
                    chunk(
                        (v_b.at[4 + i, half, rows], v_b.at[i, half, rows]),
                        (v_b.at[4 + i, half, rows], v_b.at[8 + i, half, rows]),
                    )

        send_blocks(0, shrink1(r1), send_r)
        finish = all_rows(1, send_r, True, recv_r)
        chunks[0].start()
        chunks[1].start()
        pl.when(cycle == 0)(later.start)
        finish()
        turn[...] = recv_r[0].T
        lines(chunks)
        back_r[0] = turn[...].T
        finish = all_rows(2, back_r, False, got_r)
        chunks[13].start()
        finish()

        for x in range(16):
            piece = got_r[0, 8 * tile_of(x) : 8 * tile_of(x) + 8, :]
            got_a[1, 8 * x : 8 * x + 8, :] = exchange_parts(piece)
        ends[0] = got_a[1, pl.ds(3, 32, 4), :]
        ends[1] = got_a[1, pl.ds(0, 32, 4), :]
        whole = pair(10, (got_a.at[1], got_a.at[0]), (got_a.at[1], got_a.at[2]))
        outer = pair(11, (ends.at[0], beyond.at[0]), (ends.at[1], beyond.at[1]), 2)
        whole.start()
        outer.start()
        pl.when(cycle == 0)(later.wait)
        for side in (1, 0, 2):
            if side == 0:
                for each in chunks:
                    each.wait()
                whole.wait()
                outer.wait()
            for a in range(2):
                grown[a] = dot(got_a[side], unfold[a])
            for a in range(2):
                for b in range(2):
                    for p in range(4):
                        piece = grown[a, pl.ds(b * 4 + p, 16, 8), :]
                        for i in range(2):
                            rows = pl.ds(PAD + 4 * a + 2 * b + i, 16, 8)
                            q = 4 * side + p + 1
                            w_a[q, rows, :] = w_b[q, rows, :] + piece
        for side in range(2):
            for a in range(2):
                grown[a, 0:32, :] = dot(beyond[side], unfold[a])
                for b in range(2):
                    piece = grown[a, pl.ds(b, 16, 2), :]
                    for i in range(2):
                        rows = pl.ds(PAD + 4 * a + 2 * b + i, 16, 8)
                        w_a[13 * side, rows, :] = w_b[13 * side, rows, :] + piece
        sweep1(w_a, store_second, 4)
        sweep1(w_b, store_error, 3)

        @pl.loop(0, 10)
        def _(p):
            for half in range(2):
                piece = dot(e1[p], spread[half])
                for i in range(2):
                    rows = pl.ds(PAD + i, 128, 2)
                    v_c[p, half, rows, :] = v_b[p, half, rows, :] + piece

        sweep0(v_c, v_b, -2, 8)
        sweep0(v_b, v_a, -1, 6)
        residual0(v_a, False, cycle, 0, 4)

    stores = []
    for p in range(4):
        for half in range(2):
            stores.append(
                pltpu.make_async_copy(
                    v_a.at[p + 3, half, pl.ds(PAD, 256)],
                    out.at[p, :, pl.ds(half * 128, 128)],
                    in_sem.at[0, p, half],
                )
            )
    for copy in stores:
        copy.start()

    sums = [jnp.sum(nacc[c], axis=0, keepdims=True) for c in range(CYCLES)]
    sums = [each + roll_lanes(each, 64) for each in sums]
    first = lax.broadcasted_iota(jnp.int32, (1, 128), 1) < 64
    part[0] = jnp.broadcast_to(jnp.where(first, sums[0], sums[1]), (128, 128))
    all_rows(3, part, True, nz)()
    total = jnp.sum(nz[0], axis=0, keepdims=True)
    norms[0] = jnp.sum(jnp.where(first, total, 0.0)) * (1.0 / (512 * 256 * 256))
    norms[1] = jnp.sum(jnp.where(first, 0.0, total)) * (1.0 / (512 * 256 * 256))
    for copy in stores:
        copy.wait()


def vmem(*shape):
    return pltpu.VMEM(shape, F32)


def shards(source, vertical, reaction):
    dma = pltpu.SemaphoreType.DMA
    solved, norms = pl.pallas_call(
        kernel,
        out_shape=(
            jax.ShapeDtypeStruct((4, 256, 256), F32),
            jax.ShapeDtypeStruct((CYCLES,), F32),
        ),
        in_specs=[
            pl.BlockSpec(memory_space=pltpu.HBM),
            pl.BlockSpec(memory_space=pltpu.SMEM),
            pl.BlockSpec(memory_space=pltpu.HBM),
        ],
        out_specs=(pl.BlockSpec(memory_space=pltpu.HBM), pl.BlockSpec(memory_space=pltpu.SMEM)),
        scratch_shapes=[
            vmem(10, 2, 256 + 2 * PAD, 128),
            vmem(10, 2, 256 + 2 * PAD, 128),
            vmem(10, 2, 256 + 2 * PAD, 128),
            vmem(10, 2, 256 + 2 * PAD, 128),
            vmem(8, 2, 256, 128),
            vmem(4, 2, 256, 128),
            vmem(8, 2, 256, 128),
            vmem(4, 2, 256, 128),
            vmem(12, 8, 128),
            vmem(14, 128 + 2 * PAD, 128),
            vmem(14, 128 + 2 * PAD, 128),
            vmem(12, 128, 128),
            vmem(4, 128, 128),
            vmem(12, 128, 128),
            vmem(4, 128, 128),
            vmem(10, 128, 128),
            pltpu.VMEM((2, 128, 128), jnp.bfloat16),
            pltpu.VMEM((2, 128, 128), jnp.bfloat16),
            vmem(2, 128, 128),
            pltpu.VMEM((2, 128, 128), jnp.bfloat16),
            pltpu.VMEM((2, 128, 128), jnp.bfloat16),
            vmem(2, 128, 128),
            vmem(2, 128, 128),
            vmem(1, 128, 128),
            vmem(1, 128, 128),
            vmem(128, 128),
            vmem(1, 128, 128),
            vmem(1, 128, 128),
            vmem(3, 128, 128),
            vmem(2, 32, 128),
            vmem(2, 32, 128),
            vmem(2, 128, 128),
            vmem(7, 32, 128),
            vmem(2, 32, 128),
            vmem(7, 2 * STEPS + 1, 32, 128),
            vmem(EVENTS, 128, 128),
            vmem(EVENTS, 2, 32, 128),
            vmem(EVENTS, 2, 16, 128),
            vmem(EVENTS, 2, 16, 128),
            vmem(4, 32, 128),
            vmem(2, 32, 128),
            vmem(2, 32, 128),
            vmem(CYCLES, 8, 128),
            vmem(1, 128, 128),
            vmem(1, 128, 128),
            dma((2, 4, 2)),
            dma((13, 2)),
            dma((13, 2)),
            dma((14, 2)),
            dma((14, 2)),
            dma((4,)),
            dma((4,)),
            dma((EVENTS, 4)),
            dma((EVENTS, 4)),
        ],
        compiler_params=pltpu.CompilerParams(
            collective_id=0, has_side_effects=True, vmem_limit_bytes=63 * 1024 * 1024
        ),
    )(source, vertical, reaction)
    return solved, norms


def solution(mesh):
    planes = P(("gz", "gy"), None, None)
    return jax.shard_map(
        shards,
        mesh=mesh,
        in_specs=(planes, P(("gz", "gy")), planes),
        out_specs=(planes, P()),
        check_vma=False,
    )
```

time: 244 us -> 225 us (0.922)
  Pallas kernels: 238 us -> 221 us
    pallas_call x1, Pallas kernels: 238 us -> 221 us  [shards(): pl.pallas_call(kernel, out_shape=(jax.ShapeDtypeStruct((4, 256, 256), F32...]
where the time goes in v3:
time: 225 us
  Pallas kernels  221 us (98%)
  local copies, waits for them, and re-layouts  2.8 us (1%)
    pallas_call x1, Pallas kernels, shards(): pl.pallas_call(kernel, out_shape=(jax.ShapeDtypeStruct((4, 256, 256), F32...  221 us

profile of v3, /device:TPU:1, one launch (start us, length us, event | category | flops | bytes accessed | tf_op | source)
XLA Modules:
  0.0 224.7 jit_solution(11393224301516580603)
XLA Ops:
  0.6 221.2 %shard_map.50 = (f32[4,256,256]{2,1,0:T(8,128)}, f32[2]{0:T(128)}) custom-call(f32[4,256,256]{2,1,0:T(8,128)} %source.1, f32[4]{0:T(128)} %vertical.1, f32[4,256,256]{2,1,0:T(8,128)} %reaction.1), custom_call_target="tpu_custom_call" | custom-call | tf_op jit(solution)/shard_map/pallas_call | solution.py:807
  221.8 0.0 copy-start
  221.9 2.3 %copy.7 = f32[4,256,256]{2,1,0:T(8,128)} copy(f32[4,256,256]{2,1,0:T(8,128)} %get-tuple-element.4) | data formatting | bytes 2097152
  224.1 0.0 copy-done
  224.1 0.5 copy.8
Async XLA Ops:
  221.8 2.3 %copy-start = (f32[2]{0:T(128)S(1)}, f32[2]{0:T(128)}, u32[]{:S(2)}) copy-start(f32[2]{0:T(128)} %get-tuple-element.5) | copy-start | bytes 28

commit v4 on v3

--- a/solution.py
+++ b/solution.py
@@ -18,6 +18,7 @@
 GROUP_Y = 8
 DEVICES = 128
 PAD = 8
+PLAN = {0: (2,), 1: (3,), 2: (4,), 4: (5,), 6: (6,), 8: (7,), 9: (8,), 10: (9,)}
 
 
 def device_of(a, b):
@@ -109,10 +110,10 @@
     source, vertical, reaction, out, norms,
     v_a, v_b, v_c, v_d, g0, d0, j0, r0, vt, w_a, w_b, g1, d1, j1, r1, e1, compact, spread, lhs,
     fold, unfold, send_s, recv_s, send_r, recv_r, turn, back_r, got_r, got_a, beyond, ends, grown,
-    dl, vl, cf, val, hx, hy, ys, rhs2, rhs3, res,
+    dl, vl, cf, val, hx, hy, ys, rhs2, rhs3, res, give, take,
     nacc, part, nz,
     in_sem, z_send, z_recv, c_send, c_recv,
-    all_send, all_recv, h_send, h_recv,
+    all_send, all_recv, p_send, p_recv, turns, h_send, h_recv,
 ):
     gz, gy = lax.axis_index("gz"), lax.axis_index("gy")
     me = gz * GROUP_Y + gy
@@ -217,15 +218,18 @@
         for e in range(EVENTS):
             hx[e, 1] = jnp.zeros((32, 128), F32)
 
-    @pl.when(narrow == 0)
-    def _():
-        for e in range(EVENTS):
-            hy[e, 0] = jnp.zeros((16, 128), F32)
-
-    @pl.when(narrow == GROUP_Y - 1)
-    def _():
-        for e in range(EVENTS):
-            hy[e, 1] = jnp.zeros((16, 128), F32)
+    place_y = lax.rem(ib, 4)
+    for side in range(2):
+
+        @pl.when(narrow == (GROUP_Y - 1) * side)
+        def _(side=side):
+            for e in (0, 1, 9, 10):
+                hy[e, side] = jnp.zeros((16, 128), F32)
+
+        @pl.when(jnp.logical_and(core == 1, place_y == 3 * side))
+        def _(side=side):
+            for e in range(2, 9):
+                hy[e, side] = jnp.zeros((16, 128), F32)
 
     from_lane = lax.broadcasted_iota(jnp.int32, (128, 128), 0)
     to_lane = lax.broadcasted_iota(jnp.int32, (128, 128), 1)
@@ -494,7 +498,31 @@
         vl[0, tile(p), :] = jnp.where(lane == 0, 0.0, couplings[p]) if p == 0 else couplings[p]
         vl[1, tile(p), :] = jnp.where(lane == 127, 0.0, couplings[p]) if p == 3 else couplings[p]
     react2 = unpack(recv_s[0].T)
-    react3 = shrink2(react2)
+    own_row = row % 2 == lax.rem(narrow, 2)
+
+    def to_partner(i):
+        return pltpu.make_async_remote_copy(
+            src_ref=give.at[i], dst_ref=take.at[i], send_sem=p_send.at[i], recv_sem=p_recv.at[i],
+            device_id=device_of(ia, lax.rem(ib + 4, GROUP_Y)), device_id_type=MESH,
+        )
+
+    def merge(i, v):
+        for x in range(2):
+            for p in range(4):
+                give[i, tile(4 * x + p), :] = v[x][p]
+        copy = to_partner(i)
+        copy.start()
+        copy.wait()
+        return [
+            [jnp.where(own_row, v[x][p], take[i, tile(4 * x + p), :]) for p in range(4)]
+            for x in range(2)
+        ]
+
+    def unmerge(v):
+        shifted = jnp.where(lax.rem(narrow, 2) == 0, roll_rows(v, 1), roll_rows(v, -1))
+        return jnp.where(own_row, v, shifted)
+
+    react3 = merge(0, shrink2(react2))
     react4 = shrink3(react3)
     order = [(2, each) for each in react2] + [(3, each) for each in react3] + [(4, react4[0])]
     for i, (level, lines) in enumerate(order):
@@ -503,42 +531,67 @@
 
     @pl.loop(0, 7)
     def _(i):
-        low = [-vl[0, tile(g), :] for g in range(4)]
-        high = [-vl[1, tile(g), :] for g in range(4)]
-        middle = [dl[i, tile(g), :] for g in range(4)]
-        for k in range(STEPS):
-            s = 1 << k
-            middle_below, middle_above = below(middle, s), above(middle, s)
-            left = [-low[g] / middle_below[g] for g in range(4)]
-            right = [-high[g] / middle_above[g] for g in range(4)]
-            for g in range(4):
-                cf[i, 2 * k, tile(g), :] = left[g]
-                cf[i, 2 * k + 1, tile(g), :] = right[g]
-            high_below, low_above = below(high, s), above(low, s)
-            middle = [middle[g] + left[g] * high_below[g] + right[g] * low_above[g] for g in range(4)]
-            if k < STEPS - 1:
-                low_below, high_above = below(low, s), above(high, s)
-                low = [left[g] * low_below[g] for g in range(4)]
-                high = [right[g] * high_above[g] for g in range(4)]
-        for g in range(4):
-            cf[i, 2 * STEPS, tile(g), :] = 1.0 / middle[g]
+        def put(n, v):
+            cf[i, tile(n), :] = v
+
+        def next_lane(v):
+            return roll_lanes(v, -1)
+
+        a = [-vl[0, tile(p), :] for p in range(4)]
+        c = [-vl[1, tile(p), :] for p in range(4)]
+        b = [dl[i, tile(p), :] for p in range(4)]
+        left1, right1 = -a[1] / b[0], -c[1] / b[2]
+        left3, right3 = -a[3] / b[2], -c[3] / next_lane(b[0])
+        b1 = b[1] + left1 * c[0] + right1 * a[2]
+        a1, c1 = left1 * a[0], right1 * c[2]
+        b3 = b[3] + left3 * c[2] + right3 * next_lane(a[0])
+        a3, c3 = left3 * a[2], right3 * next_lane(c[0])
+        for n, v in enumerate((left1, right1, left3, right3)):
+            put(n, v)
+        left, right = -a3 / b1, -c3 / next_lane(b1)
+        put(4, left)
+        put(5, right)
+        middle = b3 + left * c1 + right * next_lane(a1)
+        low, high = left * a1, right * next_lane(c1)
+        for k in range(STEPS - 2):
+            t = 1 << k
+            left = -low / roll_lanes(middle, t)
+            right = -high / roll_lanes(middle, -t)
+            put(6 + 2 * k, left)
+            put(7 + 2 * k, right)
+            middle = middle + left * roll_lanes(high, t) + right * roll_lanes(low, -t)
+            low, high = left * roll_lanes(low, t), right * roll_lanes(high, -t)
+        put(20, 1.0 / middle)
+        for n, (below_it, it, above_it) in enumerate(((a1, b1, c1), (a[0], b[0], c[0]), (a[2], b[2], c[2]))):
+            inverse = 1.0 / it
+            put(21 + 3 * n, inverse)
+            put(22 + 3 * n, below_it * inverse)
+            put(23 + 3 * n, above_it * inverse)
 
     first_of = {2: 0, 3: 4, 4: 6}
     count_of = {2: 4, 3: 2, 4: 1}
 
     def solve(level, right):
         solved = []
-        for a in range(count_of[level]):
-            i = first_of[level] + a
-            r = right[a]
-            for k in range(STEPS):
-                s = 1 << k
-                down, up = below(r, s), above(r, s)
-                r = [
-                    r[g] + cf[i, 2 * k, tile(g), :] * down[g] + cf[i, 2 * k + 1, tile(g), :] * up[g]
-                    for g in range(4)
-                ]
-            solved.append([r[g] * cf[i, 2 * STEPS, tile(g), :] for g in range(4)])
+        for x in range(count_of[level]):
+            i = first_of[level] + x
+
+            def at(n, i=i):
+                return cf[i, tile(n), :]
+
+            r0_, r1_, r2_, r3_ = right[x]
+            odd = r1_ + at(0) * r0_ + at(1) * r2_
+            r = r3_ + at(2) * r2_ + at(3) * roll_lanes(r0_, -1)
+            r = r + at(4) * odd + at(5) * roll_lanes(odd, -1)
+            for k in range(STEPS - 2):
+                t = 1 << k
+                r = r + at(6 + 2 * k) * roll_lanes(r, t) + at(7 + 2 * k) * roll_lanes(r, -t)
+            w3 = r * at(20)
+            before = roll_lanes(w3, 1)
+            w1 = odd * at(21) - at(22) * before - at(23) * w3
+            w0 = r0_ * at(24) - at(25) * before - at(26) * w1
+            w2 = r2_ * at(27) - at(28) * w1 - at(29) * w3
+            solved.append([w0, w1, w2, w3])
         return solved
 
     def around(level, event, v, chunks):
@@ -550,12 +603,18 @@
         ys[event, 0, 0:size, :] = val[event, pl.ds(0, size, 8), :]
         ys[event, 1, 0:size, :] = val[event, pl.ds(7, size, 8), :]
         span = pl.ds(0, size)
+        if level == 2:
+            above_y, below_y = member_narrow(narrow + 1), member_narrow(narrow - 1)
+            has_y = (narrow < GROUP_Y - 1, narrow > 0)
+        else:
+            above_y, below_y = ib + 1, ib - 1
+            has_y = (place_y < 3, place_y > 0)
         copies = []
         for side, src, dst, there in (
             (0, val.at[event, pl.ds(32 * (count - 1), 32)], hx.at[event, 0], device_of(member_wide(wide + 1), ib)),
             (1, val.at[event, pl.ds(0, 32)], hx.at[event, 1], device_of(member_wide(wide - 1), ib)),
-            (2, ys.at[event, 1, span], hy.at[event, 0, span], device_of(ia, member_narrow(narrow + 1))),
-            (3, ys.at[event, 0, span], hy.at[event, 1, span], device_of(ia, member_narrow(narrow - 1))),
+            (2, ys.at[event, 1, span], hy.at[event, 0, span], device_of(ia, above_y)),
+            (3, ys.at[event, 0, span], hy.at[event, 1, span], device_of(ia, below_y)),
         ):
             copies.append(
                 pltpu.make_async_remote_copy(
@@ -563,14 +622,35 @@
                     recv_sem=h_recv.at[event, side], device_id=there, device_id_type=MESH,
                 )
             )
-        has = (wide < GROUP_Z - 1, wide > 0, narrow < GROUP_Y - 1, narrow > 0)
+        has = (wide < GROUP_Z - 1, wide > 0) + has_y
         for side in range(4):
             pl.when(has[side])(copies[side].start)
-        chunks[event + 2].start()
+        for n in PLAN.get(event, ()):
+            chunks[n].start()
+        if level > 2:
+            pl.semaphore_signal(
+                turns.at[event], inc=1, device_id=device_of(ia, lax.rem(ib + 4, GROUP_Y)),
+                device_id_type=MESH,
+            )
         for side in range(4):
             pl.when(has[side])(copies[side].wait_send)
             pl.when(has[side])(copies[side ^ 1].wait_recv)
-        shift = 1 << (level - 2)
+
+        def beside(mine, low, high):
+            def rolled(s):
+                return roll_rows(mine, s)
+
+            if level == 2:
+                return jnp.where(row < 1, low, rolled(1)) + jnp.where(row >= 7, high, rolled(-1))
+            if level == 3:
+                before = jnp.where(row == 0, low, jnp.where(row == 1, rolled(3), rolled(2)))
+                after = jnp.where(row == 7, high, jnp.where(row == 6, rolled(-3), rolled(-2)))
+                return before + after
+            even = row % 2 == 0
+            before = jnp.where(row >= 4, rolled(4), jnp.where(even, low, rolled(-3)))
+            after = jnp.where(row < 4, rolled(4), jnp.where(even, rolled(3), high))
+            return before + after
+
         result = []
         for x in range(count):
             mine = []
@@ -579,9 +659,7 @@
                 total = total + (v[x + 1][p] if x + 1 < count else hx[event, 1, tile(p), :])
                 low = jnp.broadcast_to(hy[event, 0, pl.ds(x * 4 + p, 1), :], (8, 128))
                 high = jnp.broadcast_to(hy[event, 1, pl.ds(x * 4 + p, 1), :], (8, 128))
-                total = total + jnp.where(row < shift, low, roll_rows(v[x][p], shift))
-                total = total + jnp.where(row >= 8 - shift, high, roll_rows(v[x][p], -shift))
-                mine.append(total)
+                mine.append(total + beside(v[x][p], low, high))
             result.append(mine)
         return result
 
@@ -619,20 +697,40 @@
         v = relax(2, target2(), around(2, 0, v, chunks))
         r = residual(2, target2(), v, around(2, 1, v, chunks))
         keep(rhs2, v)
-        keep(rhs3, shrink2(r))
-        target3 = lambda: load(rhs3, 2)
-        v = solve(3, target3())
-        v = relax(3, target3(), around(3, 2, v, chunks))
-        r = residual(3, target3(), v, around(3, 3, v, chunks))
-        keep(res, v)
-        target4 = shrink3(r)
-        v = solve(4, target4)
-        for e in range(3):
-            v = relax(4, target4, around(4, 4 + e, v, chunks))
-        w = load(res, 2)
-        v = [[w[a][g] + v[0][g] for g in range(4)] for a in range(2)]
-        v = relax(3, target3(), around(3, 7, v, chunks))
-        v = relax(3, target3(), around(3, 8, v, chunks))
+        keep(rhs3, merge(1, shrink2(r)))
+        back = to_partner(2)
+
+        @pl.when(core == 0)
+        def _():
+            for e in range(2, 9):
+                pl.semaphore_wait(turns.at[e], 1)
+                for n in PLAN.get(e, ()):
+                    chunks[n].start()
+            back.wait_recv()
+
+        @pl.when(core == 1)
+        def _():
+            target3 = lambda: load(rhs3, 2)
+            v = solve(3, target3())
+            v = relax(3, target3(), around(3, 2, v, chunks))
+            r = residual(3, target3(), v, around(3, 3, v, chunks))
+            keep(res, v)
+            target4 = shrink3(r)
+            v = solve(4, target4)
+            for e in range(3):
+                v = relax(4, target4, around(4, 4 + e, v, chunks))
+            w = load(res, 2)
+            v = [[w[a][g] + v[0][g] for g in range(4)] for a in range(2)]
+            v = relax(3, target3(), around(3, 7, v, chunks))
+            v = relax(3, target3(), around(3, 8, v, chunks))
+            for x in range(2):
+                for p in range(4):
+                    give[2, tile(4 * x + p), :] = v[x][p]
+                    take[2, tile(4 * x + p), :] = v[x][p]
+            back.start()
+            back.wait_send()
+
+        v = [[unmerge(take[2, tile(4 * x + p), :]) for p in range(4)] for x in range(2)]
         w = load(rhs2, 4)
         v = [[w[x][p] + v[x // 2][p] for p in range(4)] for x in range(4)]
         v = relax(2, target2(), around(2, 9, v, chunks))
@@ -715,12 +813,15 @@
         finish = all_rows(1, send_r, True, recv_r)
         chunks[0].start()
         chunks[1].start()
+        chunks[10].start()
         pl.when(cycle == 0)(later.start)
         finish()
         turn[...] = recv_r[0].T
         lines(chunks)
         back_r[0] = turn[...].T
         finish = all_rows(2, back_r, False, got_r)
+        chunks[11].start()
+        chunks[12].start()
         chunks[13].start()
         finish()
 
@@ -851,7 +952,7 @@
             vmem(2, 128, 128),
             vmem(7, 32, 128),
             vmem(2, 32, 128),
-            vmem(7, 2 * STEPS + 1, 32, 128),
+            vmem(7, 240, 128),
             vmem(EVENTS, 128, 128),
             vmem(EVENTS, 2, 32, 128),
             vmem(EVENTS, 2, 16, 128),
@@ -859,6 +960,8 @@
             vmem(4, 32, 128),
             vmem(2, 32, 128),
             vmem(2, 32, 128),
+            vmem(3, 64, 128),
+            vmem(3, 64, 128),
             vmem(CYCLES, 8, 128),
             vmem(1, 128, 128),
             vmem(1, 128, 128),
@@ -869,6 +972,9 @@
             dma((14, 2)),
             dma((4,)),
             dma((4,)),
+            dma((3,)),
+            dma((3,)),
+            pltpu.SemaphoreType.REGULAR((9,)),
             dma((EVENTS, 4)),
             dma((EVENTS, 4)),
         ],

time: 225 us -> 221 us (0.982)
  Pallas kernels: 221 us -> 218 us
    pallas_call x1, Pallas kernels: 221 us -> 218 us  [shards(): pl.pallas_call(kernel, out_shape=(jax.ShapeDtypeStruct((4, 256, 256), F32...]
where the time goes in v4:
time: 221 us
  Pallas kernels  218 us (99%)
  local copies, waits for them, and re-layouts  2.8 us (1%)
    pallas_call x1, Pallas kernels, shards(): pl.pallas_call(kernel, out_shape=(jax.ShapeDtypeStruct((4, 256, 256), F32...  218 us

profile of v4, /device:TPU:1, one launch (start us, length us, event | category | flops | bytes accessed | tf_op | source)
XLA Modules:
  0.0 221.0 jit_solution(4617286173722949320)
XLA Ops:
  0.6 217.5 %shard_map.50 = (f32[4,256,256]{2,1,0:T(8,128)}, f32[2]{0:T(128)}) custom-call(f32[4,256,256]{2,1,0:T(8,128)} %source.1, f32[4]{0:T(128)} %vertical.1, f32[4,256,256]{2,1,0:T(8,128)} %reaction.1), custom_call_target="tpu_custom_call" | custom-call | tf_op jit(solution)/shard_map/pallas_call | solution.py:908
  218.2 0.0 copy-start
  218.2 2.3 %copy.7 = f32[4,256,256]{2,1,0:T(8,128)} copy(f32[4,256,256]{2,1,0:T(8,128)} %get-tuple-element.4) | data formatting | bytes 2097152
  220.5 0.0 copy-done
  220.5 0.5 copy.8
Async XLA Ops:
  218.2 2.3 %copy-start = (f32[2]{0:T(128)S(1)}, f32[2]{0:T(128)}, u32[]{:S(2)}) copy-start(f32[2]{0:T(128)} %get-tuple-element.5) | copy-start | bytes 28

commit v5 on v4

--- a/solution.py
+++ b/solution.py
@@ -18,7 +18,7 @@
 GROUP_Y = 8
 DEVICES = 128
 PAD = 8
-PLAN = {0: (2,), 1: (3,), 2: (4,), 4: (5,), 6: (6,), 8: (7,), 9: (8,), 10: (9,)}
+PLAN = {0: (2,), 1: (3,), 3: (4,), 5: (5,), 7: (6,), 9: (7,), 10: (8,)}
 
 
 def device_of(a, b):
@@ -820,6 +820,7 @@
         lines(chunks)
         back_r[0] = turn[...].T
         finish = all_rows(2, back_r, False, got_r)
+        chunks[9].start()
         chunks[11].start()
         chunks[12].start()
         chunks[13].start()

time: 221 us -> 220 us (level)
  no operation moved by 1% of the time
where the time goes in v5:
time: 220 us
  Pallas kernels  217 us (99%)
  local copies, waits for them, and re-layouts  2.8 us (1%)
    pallas_call x1, Pallas kernels, shards(): pl.pallas_call(kernel, out_shape=(jax.ShapeDtypeStruct((4, 256, 256), F32...  217 us

profile of v5, /device:TPU:1, one launch (start us, length us, event | category | flops | bytes accessed | tf_op | source)
XLA Modules:
  0.0 220.0 jit_solution(18321448823114539337)
XLA Ops:
  0.6 216.5 %shard_map.50 = (f32[4,256,256]{2,1,0:T(8,128)}, f32[2]{0:T(128)}) custom-call(f32[4,256,256]{2,1,0:T(8,128)} %source.1, f32[4]{0:T(128)} %vertical.1, f32[4,256,256]{2,1,0:T(8,128)} %reaction.1), custom_call_target="tpu_custom_call" | custom-call | tf_op jit(solution)/shard_map/pallas_call | solution.py:909
  217.2 0.0 copy-start
  217.2 2.3 %copy.7 = f32[4,256,256]{2,1,0:T(8,128)} copy(f32[4,256,256]{2,1,0:T(8,128)} %get-tuple-element.4) | data formatting | bytes 2097152
  219.5 0.0 copy-done
  219.5 0.5 copy.8
Async XLA Ops:
  217.2 2.3 %copy-start = (f32[2]{0:T(128)S(1)}, f32[2]{0:T(128)}, u32[]{:S(2)}) copy-start(f32[2]{0:T(128)} %get-tuple-element.5) | copy-start | bytes 28
